TPU v7x, 8 devices: a whole 2x2x1 slice. The times are simulated.
8 devices in a mesh: tp: 1 (over z), cp: 8 (over y, x, core).
Axes of the slice: x: 2, y: 2, z: 1, core: 2. Of those that a mesh axis runs over, the one named last changes fastest.
Arguments:
- query: bfloat16 [32, 256, 4, 128], P(None, 'cp', 'tp')
- out_act: bfloat16 [32, 256, 4, 128], P(None, 'cp', 'tp')
- out_grad: bfloat16 [32, 256, 4, 128], P(None, 'cp', 'tp')
- row_lse: float32 [32, 256, 4], P(None, 'cp', 'tp')
- key_act: bfloat16 [8704, 1, 128], P('cp', 'tp')
- value_act: bfloat16 [8704, 1, 128], P('cp', 'tp')
- doc_ids: int32 [8704], replicated
Outputs:
- output 1: bfloat16 [32, 256, 4, 128], P(None, 'cp', 'tp')
- output 2: float32 [8704, 1, 128], P('cp', 'tp')
- output 3: float32 [8704, 1, 128], P('cp', 'tp')
All inputs are finite; a program needn't handle non-finite values.
Results may differ from a plain program's by a relative error of at most 0.001.
Values are sent between devices in bfloat16 or wider.
A program may use at most 1 GiB of HBM per device.

v0:
```python
import functools

import jax
import jax.numpy as jnp
from jax import lax
from jax.experimental import pallas as pl
from jax.experimental.pallas import tpu as pltpu
from jax.sharding import PartitionSpec as P


LOG2E = 1.4426950408889634
NT = (((1,), (1,)), ((), ()))
MESH = pl.DeviceIdType.MESH
VMEM, SMEM = pltpu.VMEM, pltpu.SMEM
HIGHEST = lax.Precision.HIGHEST
KT = 256
UNROLL = 4


def flip(me, bit):
    return me + bit - 2 * bit * lax.rem(me // bit, 2)


def gather_kernel(k_ref, v_ref, q_ref, do_ref, o_ref, lse_ref, ids_ref,
                  kx_ref, vx_ref, ky_ref, vy_ref, kd_ref, vd_ref, q2_ref, do2_ref, lse2_ref, delta_ref, start_ref, first_ref,
                  o2_ref, lraw_ref, mark_ref, send_sem, recv_sem, load_sem, *, pre, sub_len, loc, heads):
    me = lax.axis_index('cp')
    core = lax.rem(me, 2)
    nx, ny, nc = flip(me, 2), flip(me, 4), flip(me, 1)
    barrier = pltpu.get_barrier_semaphore()
    for other in (nx, ny, nc):
        pl.semaphore_signal(barrier, inc=1, device_id={'cp': other}, device_id_type=MESH)
    pl.semaphore_wait(barrier, 3)

    def send(i, src, dst, to):
        copy = pltpu.make_async_remote_copy(src_ref=src, dst_ref=dst, send_sem=send_sem.at[i], recv_sem=recv_sem.at[i],
                                            device_id={'cp': to}, device_id_type=MESH)
        copy.start()
        return copy

    c_kx = send(0, k_ref, kx_ref, nx)
    c_vy = send(1, v_ref, vy_ref, ny)
    c_o = send(4, o_ref, o2_ref.at[core], nc)
    c_do = send(5, do_ref, do2_ref.at[core], nc)
    c_lse = send(6, lse_ref, lraw_ref.at[core], nc)
    c_q = send(7, q_ref, q2_ref.at[core], nc)
    c_vx = send(2, v_ref, vx_ref, nx)
    c_ky = send(3, k_ref, ky_ref, ny)

    loads = [pltpu.make_async_copy(s, r.at[core], load_sem.at[i])
             for i, (s, r) in enumerate([(do_ref, do2_ref), (o_ref, o2_ref), (lse_ref, lraw_ref), (q_ref, q2_ref)])]
    for load in loads:
        load.start()

    n_rows = ids_ref.shape[0]
    n_sub = lraw_ref.shape[1]
    pad = mark_ref.shape[0]
    mark_ref[...] = jnp.zeros_like(mark_ref)
    mark_ref[0:n_rows, :] = ids_ref[...]
    ids = mark_ref[...]
    lane = lax.broadcasted_iota(jnp.int32, (pad, 128), 1)
    row = lax.broadcasted_iota(jnp.int32, (pad, 128), 0)
    prev = pltpu.roll(ids, 1, axis=1)
    prev = jnp.where(lane == 0, pltpu.roll(prev, 1, axis=0), prev)
    acc = jnp.where(ids != prev, row * 128 + lane, 0)
    for sh in (1, 2, 4, 8, 16, 32, 64):
        acc = jnp.maximum(acc, jnp.where(lane >= sh, pltpu.roll(acc, sh, axis=1), 0))
    carry = jnp.max(acc, axis=1, keepdims=True) + jnp.zeros((pad, 128), jnp.int32)
    carry = jnp.where(row >= 1, pltpu.roll(carry, 1, axis=0), 0)
    sh = 1
    while sh < pad:
        carry = jnp.maximum(carry, jnp.where(row >= sh, pltpu.roll(carry, sh, axis=0), 0))
        sh *= 2
    starts = jnp.maximum(acc, carry).astype(jnp.float32)

    def hdot(a, b, dims=None):
        dims = (((1,), (0,)), ((), ())) if dims is None else dims
        return lax.dot_general(a, b, dims, precision=HIGHEST, preferred_element_type=jnp.float32)

    per = sub_len // 128
    off = (me // 2) * 2 * loc
    r_sub = lax.broadcasted_iota(jnp.int32, (n_sub, pad), 0)
    r_row = lax.broadcasted_iota(jnp.int32, (n_sub, pad), 1)
    pick = jnp.where(r_row == pre // 128 + per * r_sub + off // 128, 1.0, 0.0)
    sub_starts = hdot(pick, starts)
    src = lax.broadcasted_iota(jnp.int32, (128, 128), 0)
    dst = lax.broadcasted_iota(jnp.int32, (128, 128), 1)
    for e in range(2):
        spread = jnp.where(src == lax.rem(off, 128) + e * loc + dst // heads, 1.0, 0.0)
        rows_start = hdot(sub_starts, spread)
        start_ref[e] = rows_start.astype(jnp.int32)
        if e == 0:
            head = jnp.where(lax.broadcasted_iota(jnp.int32, (8, 128), 1) == 0, 1.0, 0.0)
            first_ref[...] = hdot(head, rows_start, NT).astype(jnp.int32)

    def delta_of(e, o_part):
        def body(t, c):
            r0 = pl.multiple_of(t * 128, 128)
            prod = do2_ref[e, pl.ds(r0, 128), :].astype(jnp.float32) * o_part[pl.ds(r0, 128), :].astype(jnp.float32)
            delta_ref[e, pl.ds(t, 1), :] = jnp.sum(prod.T, axis=0, keepdims=True)
            return c

        lax.fori_loop(0, n_sub, body, 0)

    for load in loads:
        load.wait()
    delta_of(core, o2_ref.at[core])
    c_o.wait_recv()
    c_do.wait_recv()
    delta_of(1 - core, o2_ref.at[1 - core])
    c_kx.wait_recv()
    c_kd = send(8, kx_ref, kd_ref, ny)
    c_vy.wait_recv()
    c_vd = send(9, vy_ref, vd_ref, nx)
    c_lse.wait_recv()
    tok = lax.broadcasted_iota(jnp.int32, (loc, 128), 0)
    tok_lane = lax.broadcasted_iota(jnp.int32, (loc, 128), 1)
    tok_spread = jnp.where(tok == tok_lane // heads, 1.0, 0.0)
    head_of = lax.broadcasted_iota(jnp.int32, (n_sub * heads, 128), 0)
    head_lane = lax.broadcasted_iota(jnp.int32, (n_sub * heads, 128), 1)
    own_head = lax.rem(head_of, heads) == lax.rem(head_lane, heads)
    g_sub = lax.broadcasted_iota(jnp.int32, (n_sub, n_sub * heads), 0)
    g_row = lax.broadcasted_iota(jnp.int32, (n_sub, n_sub * heads), 1)
    group = jnp.where(g_row // heads == g_sub, 1.0, 0.0)
    for e in range(2):
        wide = hdot(lraw_ref[e].reshape(n_sub * heads, loc), tok_spread)
        lse2_ref[e] = hdot(group, jnp.where(own_head, wide, 0.0)) * LOG2E
    c_q.wait_recv()
    c_vx.wait_recv()
    c_ky.wait_recv()
    c_kd.wait_recv()
    c_vd.wait_recv()
    for copy in (c_kx, c_vy, c_vx, c_ky, c_o, c_do, c_lse, c_q, c_kd, c_vd):
        copy.wait_send()


def attn_kernel(*refs, owner_bits, has_dq, finish, scale, pre, sub_len, loc, heads):
    n_in = 9 if has_dq else 8
    first_ref, q_ref, do_ref, lse_ref, delta_ref, start_ref, k_ref, v_ref = refs[:8]
    if finish:
        own_ref, other_ref, dk_ref, dv_ref, dq_ref = refs[n_in:n_in + 5]
        it_t, it_k, it_lo = refs[n_in + 5:]
    else:
        dq_ref, dk_ref, dv_ref = refs[n_in:n_in + 3]
        it_t, it_k, it_lo = refs[n_in + 3:]
    me = lax.axis_index('cp')
    core = lax.rem(me, 2)
    owner = me
    for bit in owner_bits:
        owner = flip(owner, bit)
    blk = k_ref.shape[0]
    n_sub, half = lse_ref.shape[1], lse_ref.shape[2]
    rows = 2 * half
    blo = owner * blk
    pos0 = pre + (me // 2) * 2 * loc
    dk_ref[...] = jnp.zeros_like(dk_ref)
    dv_ref[...] = jnp.zeros_like(dv_ref)
    if finish:
        dq_ref[...] = refs[8][...]
    elif has_dq:
        dq_ref[...] = refs[8][...]
    else:
        dq_ref[...] = jnp.zeros_like(dq_ref)

    def add_tile(t, n):
        lo = jnp.maximum(first_ref[0, t], blo)
        hi = jnp.minimum(pos0 + t * sub_len + 2 * loc - 1, blo + blk - 1)
        off = (lo - blo) // 16 * 16
        cnt = jnp.where(hi >= lo, (hi - blo - off) // KT + 1, 0)

        def add_item(i, m):
            it_t[m] = t
            it_k[m] = jnp.minimum(off + i * KT, blk - KT)
            it_lo[m] = blo + off + i * KT
            return m + 1

        return lax.fori_loop(0, cnt, add_item, n)

    n_items = lax.fori_loop(0, n_sub, add_tile, 0)
    for u in range(UNROLL - 1):
        it_t[n_items + u] = 0
        it_k[n_items + u] = 0
        it_lo[n_items + u] = 1 << 30

    def two(ref, t):
        return jnp.concatenate([ref[0, pl.ds(t, 1), :], ref[1, pl.ds(t, 1), :]], axis=1)

    lane = lax.broadcasted_iota(jnp.int32, (1, rows), 1)

    def body(w, c):
        st = []
        for u in range(UNROLL):
            m = w * UNROLL + u
            t = it_t[m]
            k0 = pl.multiple_of(it_k[m], 16)
            r0 = pl.multiple_of(t * half, half)
            k = k_ref[pl.ds(k0, KT), :]
            v = v_ref[pl.ds(k0, KT), :]
            q = jnp.concatenate([q_ref[0, pl.ds(r0, half), :], q_ref[1, pl.ds(r0, half), :]], axis=0)
            do = jnp.concatenate([do_ref[0, pl.ds(r0, half), :], do_ref[1, pl.ds(r0, half), :]], axis=0)
            s = lax.dot_general(k, q, NT, preferred_element_type=jnp.float32)
            dp = lax.dot_general(v, do, NT, preferred_element_type=jnp.float32)
            st.append((m, t, k0, k, q, do, s, dp))
        mid = []
        for u in range(UNROLL):
            m, t, k0, k, q, do, s, dp = st[u]
            lo = jnp.maximum(two(start_ref, t), it_lo[m])
            qpos = lane // heads + (pos0 + t * sub_len)
            kpos = lax.broadcasted_iota(jnp.int32, (KT, rows), 0) + (k0 + blo)
            allowed = (kpos >= lo) & (kpos <= qpos)
            p = jnp.where(allowed, jnp.exp2(s * (scale * LOG2E) - two(lse_ref, t)), 0.0)
            ds = (p * (dp - two(delta_ref, t))).astype(jnp.bfloat16)
            mid.append((p.astype(jnp.bfloat16), ds))
        for u in range(UNROLL):
            m, t, k0, k, q, do, s, dp = st[u]
            p, ds = mid[u]
            dv_ref[pl.ds(k0, KT), :] += jnp.dot(p, do, preferred_element_type=jnp.float32)
            dk_ref[pl.ds(k0, KT), :] += jnp.dot(ds, q, preferred_element_type=jnp.float32)
            dq_ref[t] += jnp.dot(k.T, ds, preferred_element_type=jnp.float32)
        return c

    lax.fori_loop(0, (n_items + UNROLL - 1) // UNROLL, body, 0)
    if finish:
        mine = pl.multiple_of(core * half, half)
        theirs = pl.multiple_of((1 - core) * half, half)

        def put(t, c):
            r0 = pl.multiple_of(t * half, half)
            own_ref[pl.ds(r0, half), :] = dq_ref[t, :, pl.ds(mine, half)].T
            other_ref[pl.ds(r0, half), :] = dq_ref[t, :, pl.ds(theirs, half)].T
            return c

        lax.fori_loop(0, n_sub, put, 0)


def solution(mesh):
    cp = mesh.shape['cp']
    q_spec = P(None, 'cp', 'tp', None)
    lse_spec = P(None, 'cp', 'tp')
    kv_spec = P('cp', 'tp', None)

    def swap(x, bits):
        return lax.ppermute(x, 'cp', [(i, i ^ bits) for i in range(cp)])

    def local_backward(query, out_act, out_grad, row_lse, key_act, value_act, doc_ids):
        n_sub, loc, heads, d = query.shape
        blk = key_act.shape[0]
        n_keys = blk * cp
        half = loc * heads
        sub_len = loc * cp
        pre = n_keys - n_sub * sub_len
        scale = d ** -0.5
        f32, bf16, i32 = jnp.float32, jnp.bfloat16, jnp.int32
        dims = dict(pre=pre, sub_len=sub_len, loc=loc, heads=heads)
        vm = pl.BlockSpec(memory_space=VMEM)
        sm = pl.BlockSpec(memory_space=SMEM)
        hbm = pl.BlockSpec(memory_space=pltpu.HBM)
        sds = jax.ShapeDtypeStruct
        k_own, v_own = key_act.reshape(blk, d), value_act.reshape(blk, d)
        pad = (n_keys // 128 + 7) // 8 * 8
        kx, vx, ky, vy, kd, vd, q2, do2, lse2, delta, start, first = pl.pallas_call(
            functools.partial(gather_kernel, **dims),
            out_shape=tuple([sds((blk, d), bf16)] * 6 + [sds((2, n_sub * half, d), bf16)] * 2
                            + [sds((2, n_sub, half), f32)] * 2 + [sds((2, n_sub, half), i32), sds((8, n_sub), i32)]),
            in_specs=[hbm] * 6 + [vm], out_specs=(vm,) * 12,
            scratch_shapes=[VMEM((2, n_sub * half, d), bf16), VMEM((2, n_sub, heads, loc), f32), VMEM((pad, 128), i32),
                            pltpu.SemaphoreType.DMA((10,)), pltpu.SemaphoreType.DMA((10,)), pltpu.SemaphoreType.DMA((4,))],
            compiler_params=pltpu.CompilerParams(collective_id=0, has_side_effects=True, vmem_limit_bytes=24 * 2 ** 20),
            name='gather_kv',
        )(k_own, v_own, query.reshape(-1, d), out_grad.reshape(-1, d), out_act.reshape(-1, d),
          row_lse.transpose(0, 2, 1), doc_ids.reshape(n_keys // 128, 128))

        cap = n_sub * (-(-blk // KT) + 1) + UNROLL
        items = [SMEM((cap,), i32)] * 3
        acc = sds((n_sub, d, 2 * half), f32)
        kv_out = sds((blk, d), f32)
        dq_out = sds((n_sub * half, d), f32)
        cost = pl.CostEstimate(flops=2 * 10 ** 9, bytes_accessed=10 ** 7, transcendentals=10 ** 6)

        def attend(bits, k, v, dq=None, finish=False):
            ins = [first, q2, do2, lse2, delta, start, k, v] + ([dq] if dq is not None else [])
            outs = (dq_out, dq_out, kv_out, kv_out) if finish else (acc, kv_out, kv_out)
            return pl.pallas_call(
                functools.partial(attn_kernel, owner_bits=bits, has_dq=dq is not None, finish=finish, scale=scale, **dims),
                out_shape=outs, in_specs=[sm] + [vm] * (len(ins) - 1), out_specs=(vm,) * len(outs),
                scratch_shapes=([VMEM((n_sub, d, 2 * half), f32)] if finish else []) + items,
                compiler_params=pltpu.CompilerParams(vmem_limit_bytes=28 * 2 ** 20),
                cost_estimate=cost, name='attn_bwd')(*ins)

        def run(bits, k, v, dq=None, finish=False):
            return attend(bits, k, v, dq, finish)

        dq, dk_d, dv_d = run((2, 4), kd, vd)
        got_ky = swap(dk_d, 2)
        got_vx = swap(dv_d, 4)
        dq, dk_x, dv_x = run((2,), kx, vx, dq)
        got_ko = swap(dk_x, 2)
        dq, dk_y, dv_y = run((4,), ky, vy, dq)
        got_vo = swap(dv_y, 4)
        dq_own, dq_other, dk_o, dv_o = run((), k_own, v_own, dq, finish=True)
        last_k = swap(dk_y + got_ky, 4)
        last_v = swap(dv_x + got_vx, 2)
        got_dq = swap(dq_other, 1)
        d_query = ((dq_own + got_dq) * scale).astype(bf16)
        d_key = (dk_o + got_ko + last_k) * scale
        d_value = dv_o + got_vo + last_v
        return d_query.reshape(query.shape), d_key.reshape(key_act.shape), d_value.reshape(value_act.shape)

    return jax.shard_map(local_backward, mesh=mesh, in_specs=(q_spec, q_spec, q_spec, lse_spec, kv_spec, kv_spec, P()), out_specs=(q_spec, kv_spec, kv_spec), check_vma=False)
```

profile of v0, /device:TPU:0, one launch (start us, length us, event | category | flops | bytes accessed | tf_op | source)
XLA Modules:
  0.0 118.7 jit_solution(7000410898691567347)
XLA Ops:
  0.6 0.0 copy-start
  0.6 0.9 copy-done
  1.6 1.0 copy-done.2
  2.5 1.2 %copy-done.4 = bf16[32,32,4,128]{3,2,1,0:T(4,128)(2,1)S(1)} copy-done((bf16[32,32,4,128]{3,2,1,0:T(4,128)(2,1)S(1)}, bf16[32,32,4,128]{3,2,1,0:T(4,128)(2,1)}, u32[]{:S(2)}) %copy-start.4) | copy-done | bytes 1048600
  3.8 1.2 %copy-done.5 = bf16[32,32,4,128]{3,2,1,0:T(4,128)(2,1)S(1)} copy-done((bf16[32,32,4,128]{3,2,1,0:T(4,128)(2,1)S(1)}, bf16[32,32,4,128]{3,2,1,0:T(4,128)(2,1)}, u32[]{:S(2)}) %copy-start.5) | copy-done | bytes 1048600
  5.0 1.2 %copy-done.6 = bf16[32,32,4,128]{3,2,1,0:T(4,128)(2,1)S(1)} copy-done((bf16[32,32,4,128]{3,2,1,0:T(4,128)(2,1)S(1)}, bf16[32,32,4,128]{3,2,1,0:T(4,128)(2,1)}, u32[]{:S(2)}) %copy-start.6) | copy-done | bytes 1048600
  6.2 0.8 copy-done.7
  7.1 0.8 copy-done.8
  7.8 23.4 %gather_kv.1 = (bf16[1088,128]{1,0:T(8,128)(2,1)S(1)}, bf16[1088,128]{1,0:T(8,128)(2,1)S(1)}, bf16[1088,128]{1,0:T(8,128)(2,1)S(1)}, bf16[1088,128]{1,0:T(8,128)...) custom-call(bf16[1088,128]{1,0:T(8,128)(2,1)S(1)} %bitcast.14, ...), custom_call_target="tpu_custom_call" | custom-call | tf_op jit(solution)/shard_map/gather_kv/pallas_call | solution.py:261
  31.2 4.8 %attn_bwd.4 = (f32[32,128,256]{2,1,0:T(8,128)S(1)}, f32[1088,128]{1,0:T(8,128)S(1)}, f32[1088,128]{1,0:T(8,128)S(1)}) custom-call(s32[8,32]{1,0:T(8,128)S(1)} %get-tuple-element.28.refs_0_, bf16[2,4096,128]{2,1,0:T(8,128)(2,1)S(1)} %get-tuple-element.29.refs_1_, bf16[2,4096,128]{2,1,0:T(8,128)(2,1)S(1)} %get-tuple-element.30.refs_2_, ...), custom_call_target="tpu_custom_call" | custom-call | flops 2000000000 | bytes 10000000 | tf_op jit(solution)/shard_map/attn_bwd/pallas_call | solution.py:283
  36.0 3.0 %collective-permute-start.5 = (f32[1088,128]{1,0:T(8,128)S(1)}, f32[1088,128]{1,0:T(8,128)S(1)}, u32[]{:S(2)}, u32[]{:S(2)}) collective-permute-start(f32[1088,128]{1,0:T(8,128)S(1)} %get-tuple-element.52), channel_id=1, source_target_pairs={{0,4},{1,5},{2,6},{3,7},{4,0},{5,1},{6,2},{7,3}} | collective-permute-start | bytes 1671176 | tf_op jit(solution)/shard_map/ppermute | solution.py:243
  39.0 5.8 %attn_bwd.5 = (f32[32,128,256]{2,1,0:T(8,128)S(1)}, f32[1088,128]{1,0:T(8,128)S(1)}, f32[1088,128]{1,0:T(8,128)S(1)}) custom-call(s32[8,32]{1,0:T(8,128)S(1)} %get-tuple-element.28.refs_0_, bf16[2,4096,128]{2,1,0:T(8,128)(2,1)S(1)} %get-tuple-element.29.refs_1_, bf16[2,4096,128]{2,1,0:T(8,128)(2,1)S(1)} %get-tuple-element.30.refs_2_, ...), custom_call_target="tpu_custom_call" | custom-call | flops 2000000000 | bytes 10000000 | tf_op jit(solution)/shard_map/attn_bwd/pallas_call | solution.py:283
  44.8 0.0 copy-start.1
  44.8 0.0 copy-start.3
  44.8 11.6 %attn_bwd.6 = (f32[32,128,256]{2,1,0:T(8,128)S(1)}, f32[1088,128]{1,0:T(8,128)S(1)}, f32[1088,128]{1,0:T(8,128)S(1)}) custom-call(s32[8,32]{1,0:T(8,128)S(1)} %get-tuple-element.28.refs_0_, bf16[2,4096,128]{2,1,0:T(8,128)(2,1)S(1)} %get-tuple-element.29.refs_1_, bf16[2,4096,128]{2,1,0:T(8,128)(2,1)S(1)} %get-tuple-element.30.refs_2_, ...), custom_call_target="tpu_custom_call" | custom-call | flops 2000000000 | bytes 10000000 | tf_op jit(solution)/shard_map/attn_bwd/pallas_call | solution.py:283
  56.4 10.9 %attn_bwd.7 = (f32[4096,128]{1,0:T(8,128)S(1)}, f32[4096,128]{1,0:T(8,128)S(1)}, f32[1088,128]{1,0:T(8,128)S(1)}, f32[1088,128]{1,0:T(8,128)S(1)}) custom-call(s32[8,32]{1,0:T(8,128)S(1)} %get-tuple-element.28.refs_0_, bf16[2,4096,128]{2,1,0:T(8,128)(2,1)S(1)} %get-tuple-element.29.refs_1_, bf16[2,4096,128]{2,1,0:T(8,128)(2,1)S(1)} %get-tuple-element.30.refs_2_, ...), custom_call_target="tpu_custom_call" | custom-call | flops 2000000000 | bytes 10000000 | tf_op jit(solution)/shard_map/attn_bwd/pallas_call | solution.py:283
  67.3 10.8 %collective-permute-start = (f32[4096,128]{1,0:T(8,128)S(1)}, f32[4096,128]{1,0:T(8,128)S(1)}, u32[]{:S(2)}, u32[]{:S(2)}) collective-permute-start(f32[4096,128]{1,0:T(8,128)S(1)} %get-tuple-element.44), channel_id=1, source_target_pairs={{0,1},{1,0},{2,3},{3,2},{4,5},{5,4},{6,7},{7,6}} | collective-permute-start | bytes 6291464 | tf_op jit(solution)/shard_map/ppermute | solution.py:243
  78.1 0.0 collective-permute-start.2
  78.1 0.0 collective-permute-start.4
  78.1 0.0 collective-permute-done.5
  78.1 0.1 add.26
  78.2 2.0 %collective-permute-start.6 = (f32[1088,128]{1,0:T(8,128)S(1)}, f32[1088,128]{1,0:T(8,128)S(1)}, u32[]{:S(2)}, u32[]{:S(2)}) collective-permute-start(f32[1088,128]{1,0:T(8,128)S(1)} %add.26), channel_id=1, source_target_pairs={{0,2},{1,3},{2,0},{3,1},{4,6},{5,7},{6,4},{7,5}} | collective-permute-start | bytes 1671176 | tf_op jit(solution)/shard_map/ppermute | solution.py:243
  80.2 0.0 collective-permute-start.1
  80.3 13.3 %collective-permute-done.2 = f32[1088,128]{1,0:T(8,128)S(1)} collective-permute-done((f32[1088,128]{1,0:T(8,128)S(1)}, f32[1088,128]{1,0:T(8,128)S(1)}, u32[]{:S(2)}, u32[]{:S(2)}) %collective-permute-start.2) | collective-permute-done | bytes 557088 | tf_op jit(solution)/shard_map/ppermute | solution.py:243
  93.6 0.1 add.23
  93.7 0.0 collective-permute-start.3
  93.7 11.8 %collective-permute-done.6 = f32[1088,128]{1,0:T(8,128)S(1)} collective-permute-done((f32[1088,128]{1,0:T(8,128)S(1)}, f32[1088,128]{1,0:T(8,128)S(1)}, u32[]{:S(2)}, u32[]{:S(2)}) %collective-permute-start.6) | collective-permute-done | bytes 557088 | tf_op jit(solution)/shard_map/ppermute | solution.py:243
  105.5 0.9 add_add_fusion
  106.4 10.1 %collective-permute-done.1 = f32[1088,128]{1,0:T(8,128)S(1)} collective-permute-done((f32[1088,128]{1,0:T(8,128)S(1)}, f32[1088,128]{1,0:T(8,128)S(1)}, u32[]{:S(2)}, u32[]{:S(2)}) %collective-permute-start.1) | collective-permute-done | bytes 557088 | tf_op jit(solution)/shard_map/ppermute | solution.py:243
  116.6 0.0 collective-permute-done.3
  116.6 0.9 add_multiply_fusion
  117.5 1.2 %multiply_convert_fusion = bf16[4096,128]{1,0:T(8,128)(2,1)} fusion(f32[4096,128]{1,0:T(8,128)S(1)} %get-tuple-element.43, f32[4096,128]{1,0:T(8,128)S(1)} %collective-permute-done), kind=kLoop, calls=%fused_computation | loop fusion | flops 1572864 | bytes 5242880 | tf_op jit(solution)/shard_map/convert_element_type | solution.py:304
  (10 shorter events, 0.0 us)
Async XLA Ops:
  0.6 1.0 copy-start
  1.6 1.0 copy-start.2
  2.5 1.2 %copy-start.4 = (bf16[32,32,4,128]{3,2,1,0:T(4,128)(2,1)S(1)}, bf16[32,32,4,128]{3,2,1,0:T(4,128)(2,1)}, u32[]{:S(2)}) copy-start(bf16[32,32,4,128]{3,2,1,0:T(4,128)(2,1)} %param.7) | copy-start | bytes 3145732
  3.8 1.2 %copy-start.5 = (bf16[32,32,4,128]{3,2,1,0:T(4,128)(2,1)S(1)}, bf16[32,32,4,128]{3,2,1,0:T(4,128)(2,1)}, u32[]{:S(2)}) copy-start(bf16[32,32,4,128]{3,2,1,0:T(4,128)(2,1)} %param.9) | copy-start | bytes 3145732
  5.0 1.2 %copy-start.6 = (bf16[32,32,4,128]{3,2,1,0:T(4,128)(2,1)S(1)}, bf16[32,32,4,128]{3,2,1,0:T(4,128)(2,1)}, u32[]{:S(2)}) copy-start(bf16[32,32,4,128]{3,2,1,0:T(4,128)(2,1)} %param.8) | copy-start | bytes 3145732
  6.2 0.8 copy-start.7
  7.1 0.8 copy-start.8
  36.0 42.1 %collective-permute-start.5 = (f32[1088,128]{1,0:T(8,128)S(1)}, f32[1088,128]{1,0:T(8,128)S(1)}, u32[]{:S(2)}, u32[]{:S(2)}) collective-permute-start(f32[1088,128]{1,0:T(8,128)S(1)} %get-tuple-element.52), channel_id=1, source_target_pairs={{0,4},{1,5},{2,6},{3,7},{4,0},{5,1},{6,2},{7,3}} | collective-permute-start | bytes 1671176 | tf_op jit(solution)/shard_map/ppermute | solution.py:243
  44.8 11.6 %copy-start.1 = (bf16[1088,1,128]{2,0,1:T(8,128)(2,1)S(1)}, bf16[1088,1,128]{2,0,1:T(8,128)(2,1)}, u32[]{:S(2)}) copy-start(bf16[1088,1,128]{2,0,1:T(8,128)(2,1)} %param.11) | copy-start | bytes 835588
  44.8 11.6 %copy-start.3 = (bf16[1088,1,128]{2,0,1:T(8,128)(2,1)S(1)}, bf16[1088,1,128]{2,0,1:T(8,128)(2,1)}, u32[]{:S(2)}) copy-start(bf16[1088,1,128]{2,0,1:T(8,128)(2,1)} %param.12) | copy-start | bytes 835588
  67.3 50.2 %collective-permute-start = (f32[4096,128]{1,0:T(8,128)S(1)}, f32[4096,128]{1,0:T(8,128)S(1)}, u32[]{:S(2)}, u32[]{:S(2)}) collective-permute-start(f32[4096,128]{1,0:T(8,128)S(1)} %get-tuple-element.44), channel_id=1, source_target_pairs={{0,1},{1,0},{2,3},{3,2},{4,5},{5,4},{6,7},{7,6}} | collective-permute-start | bytes 6291464 | tf_op jit(solution)/shard_map/ppermute | solution.py:243
  78.1 15.5 %collective-permute-start.2 = (f32[1088,128]{1,0:T(8,128)S(1)}, f32[1088,128]{1,0:T(8,128)S(1)}, u32[]{:S(2)}, u32[]{:S(2)}) collective-permute-start(f32[1088,128]{1,0:T(8,128)S(1)} %get-tuple-element.48), channel_id=1, source_target_pairs={{0,2},{1,3},{2,0},{3,1},{4,6},{5,7},{6,4},{7,5}} | collective-permute-start | bytes 1671176 | tf_op jit(solution)/shard_map/ppermute | solution.py:243
  78.1 15.6 %collective-permute-start.4 = (f32[1088,128]{1,0:T(8,128)S(1)}, f32[1088,128]{1,0:T(8,128)S(1)}, u32[]{:S(2)}, u32[]{:S(2)}) collective-permute-start(f32[1088,128]{1,0:T(8,128)S(1)} %get-tuple-element.50), channel_id=1, source_target_pairs={{0,4},{1,5},{2,6},{3,7},{4,0},{5,1},{6,2},{7,3}} | collective-permute-start | bytes 1671176 | tf_op jit(solution)/shard_map/ppermute | solution.py:243
  78.2 27.4 %collective-permute-start.6 = (f32[1088,128]{1,0:T(8,128)S(1)}, f32[1088,128]{1,0:T(8,128)S(1)}, u32[]{:S(2)}, u32[]{:S(2)}) collective-permute-start(f32[1088,128]{1,0:T(8,128)S(1)} %add.26), channel_id=1, source_target_pairs={{0,2},{1,3},{2,0},{3,1},{4,6},{5,7},{6,4},{7,5}} | collective-permute-start | bytes 1671176 | tf_op jit(solution)/shard_map/ppermute | solution.py:243
  80.2 36.3 %collective-permute-start.1 = (f32[1088,128]{1,0:T(8,128)S(1)}, f32[1088,128]{1,0:T(8,128)S(1)}, u32[]{:S(2)}, u32[]{:S(2)}) collective-permute-start(f32[1088,128]{1,0:T(8,128)S(1)} %get-tuple-element.46), channel_id=1, source_target_pairs={{0,2},{1,3},{2,0},{3,1},{4,6},{5,7},{6,4},{7,5}} | collective-permute-start | bytes 1671176 | tf_op jit(solution)/shard_map/ppermute | solution.py:243
  93.7 22.9 %collective-permute-start.3 = (f32[1088,128]{1,0:T(8,128)S(1)}, f32[1088,128]{1,0:T(8,128)S(1)}, u32[]{:S(2)}, u32[]{:S(2)}) collective-permute-start(f32[1088,128]{1,0:T(8,128)S(1)} %add.23), channel_id=1, source_target_pairs={{0,4},{1,5},{2,6},{3,7},{4,0},{5,1},{6,2},{7,3}} | collective-permute-start | bytes 1671176 | tf_op jit(solution)/shard_map/ppermute | solution.py:243
where the time goes:
time: 119 us
  Pallas kernels  56.4 us (47%)
  waiting for transfers between devices  35.3 us (30%)
  starting transfers between devices  15.9 us (13%)
  local copies, waits for them, and re-layouts  7.2 us (6%)
  other arithmetic  3.18 us (3%)
    ppermute x7, waiting for transfers between devices, swap(): return lax.ppermute(x, 'cp', [(i, i ^ bits) for i in range(cp)])  35.3 us
    pallas_call x4, Pallas kernels, attend(): pl.pallas_call(functools.partial(attn_kernel, owner_bits=bits, has_dq=dq...  33 us
    pallas_call x1, Pallas kernels, local_backward(): pl.pallas_call(functools.partial(gather_kernel, **dims), out_shape=tuple(...  23.4 us
    ppermute x7, starting transfers between devices, swap(): return lax.ppermute(x, 'cp', [(i, i ^ bits) for i in range(cp)])  15.9 us
    unnamed x18, local copies, waits for them, and re-layouts  7.2 us
  transfers between devices with their start and end apart: 7, of which 3 were waited for; matrix products, arithmetic and copies ran while one was open for 2% of the time, Pallas kernels for 24%

commit v1 on v0

--- a/solution.py
+++ b/solution.py
@@ -55,8 +55,10 @@
     n_rows = ids_ref.shape[0]
     n_sub = lraw_ref.shape[1]
     pad = mark_ref.shape[0]
-    mark_ref[...] = jnp.zeros_like(mark_ref)
-    mark_ref[0:n_rows, :] = ids_ref[...]
+    load_ids = pltpu.make_async_copy(ids_ref, mark_ref.at[pl.ds(0, n_rows)], load_sem.at[4])
+    load_ids.start()
+    mark_ref[pl.ds(n_rows, pad - n_rows), :] = jnp.zeros((pad - n_rows, 128), jnp.int32)
+    load_ids.wait()
     ids = mark_ref[...]
     lane = lax.broadcasted_iota(jnp.int32, (pad, 128), 1)
     row = lax.broadcasted_iota(jnp.int32, (pad, 128), 0)
@@ -134,17 +136,27 @@
         copy.wait_send()
 
 
-def attn_kernel(*refs, owner_bits, has_dq, finish, scale, pre, sub_len, loc, heads):
+def split_kernel(dq_ref, own_ref, other_ref):
+    n_sub, _, rows = dq_ref.shape
+    half = rows // 2
+    core = lax.rem(lax.axis_index('cp'), 2)
+    mine = pl.multiple_of(core * half, half)
+    theirs = pl.multiple_of((1 - core) * half, half)
+
+    def put(t, c):
+        r0 = pl.multiple_of(t * half, half)
+        other_ref[pl.ds(r0, half), :] = dq_ref[t, :, pl.ds(theirs, half)].T
+        own_ref[pl.ds(r0, half), :] = dq_ref[t, :, pl.ds(mine, half)].T
+        return c
+
+    lax.fori_loop(0, n_sub, put, 0)
+
+
+def attn_kernel(*refs, owner_bits, has_dq, scale, pre, sub_len, loc, heads):
     n_in = 9 if has_dq else 8
     first_ref, q_ref, do_ref, lse_ref, delta_ref, start_ref, k_ref, v_ref = refs[:8]
-    if finish:
-        own_ref, other_ref, dk_ref, dv_ref, dq_ref = refs[n_in:n_in + 5]
-        it_t, it_k, it_lo = refs[n_in + 5:]
-    else:
-        dq_ref, dk_ref, dv_ref = refs[n_in:n_in + 3]
-        it_t, it_k, it_lo = refs[n_in + 3:]
+    dq_ref, dk_ref, dv_ref, it_t, it_k, it_lo = refs[n_in:]
     me = lax.axis_index('cp')
-    core = lax.rem(me, 2)
     owner = me
     for bit in owner_bits:
         owner = flip(owner, bit)
@@ -155,18 +167,20 @@
     pos0 = pre + (me // 2) * 2 * loc
     dk_ref[...] = jnp.zeros_like(dk_ref)
     dv_ref[...] = jnp.zeros_like(dv_ref)
-    if finish:
-        dq_ref[...] = refs[8][...]
-    elif has_dq:
+    if has_dq:
         dq_ref[...] = refs[8][...]
     else:
         dq_ref[...] = jnp.zeros_like(dq_ref)
 
-    def add_tile(t, n):
+    def more(c):
+        return (c[0] < n_sub) & (first_ref[0, jnp.minimum(c[0], n_sub - 1)] < blo + blk)
+
+    def add_tile(c):
+        t, n = c
         lo = jnp.maximum(first_ref[0, t], blo)
         hi = jnp.minimum(pos0 + t * sub_len + 2 * loc - 1, blo + blk - 1)
         off = (lo - blo) // 16 * 16
-        cnt = jnp.where(hi >= lo, (hi - blo - off) // KT + 1, 0)
+        cnt = (hi - blo - off) // KT + 1
 
         def add_item(i, m):
             it_t[m] = t
@@ -174,9 +188,10 @@
             it_lo[m] = blo + off + i * KT
             return m + 1
 
-        return lax.fori_loop(0, cnt, add_item, n)
-
-    n_items = lax.fori_loop(0, n_sub, add_tile, 0)
+        return t + 1, lax.fori_loop(0, cnt, add_item, n)
+
+    t_first = jnp.maximum(blo - pos0 - 2 * loc + sub_len, 0) // sub_len
+    n_items = lax.while_loop(more, add_tile, (t_first, 0))[1]
     for u in range(UNROLL - 1):
         it_t[n_items + u] = 0
         it_k[n_items + u] = 0
@@ -220,17 +235,6 @@
         return c
 
     lax.fori_loop(0, (n_items + UNROLL - 1) // UNROLL, body, 0)
-    if finish:
-        mine = pl.multiple_of(core * half, half)
-        theirs = pl.multiple_of((1 - core) * half, half)
-
-        def put(t, c):
-            r0 = pl.multiple_of(t * half, half)
-            own_ref[pl.ds(r0, half), :] = dq_ref[t, :, pl.ds(mine, half)].T
-            other_ref[pl.ds(r0, half), :] = dq_ref[t, :, pl.ds(theirs, half)].T
-            return c
-
-        lax.fori_loop(0, n_sub, put, 0)
 
 
 def solution(mesh):
@@ -262,13 +266,14 @@
             functools.partial(gather_kernel, **dims),
             out_shape=tuple([sds((blk, d), bf16)] * 6 + [sds((2, n_sub * half, d), bf16)] * 2
                             + [sds((2, n_sub, half), f32)] * 2 + [sds((2, n_sub, half), i32), sds((8, n_sub), i32)]),
-            in_specs=[hbm] * 6 + [vm], out_specs=(vm,) * 12,
+            in_specs=[hbm] * 7, out_specs=(vm,) * 12,
             scratch_shapes=[VMEM((2, n_sub * half, d), bf16), VMEM((2, n_sub, heads, loc), f32), VMEM((pad, 128), i32),
-                            pltpu.SemaphoreType.DMA((10,)), pltpu.SemaphoreType.DMA((10,)), pltpu.SemaphoreType.DMA((4,))],
+                            pltpu.SemaphoreType.DMA((10,)), pltpu.SemaphoreType.DMA((10,)), pltpu.SemaphoreType.DMA((5,))],
             compiler_params=pltpu.CompilerParams(collective_id=0, has_side_effects=True, vmem_limit_bytes=24 * 2 ** 20),
             name='gather_kv',
-        )(k_own, v_own, query.reshape(-1, d), out_grad.reshape(-1, d), out_act.reshape(-1, d),
-          row_lse.transpose(0, 2, 1), doc_ids.reshape(n_keys // 128, 128))
+        )(*[pltpu.with_memory_space_constraint(x, pltpu.HBM) for x in (
+            k_own, v_own, query.reshape(-1, d), out_grad.reshape(-1, d), out_act.reshape(-1, d),
+            row_lse.transpose(0, 2, 1), doc_ids.reshape(n_keys // 128, 128))])
 
         cap = n_sub * (-(-blk // KT) + 1) + UNROLL
         items = [SMEM((cap,), i32)] * 3
@@ -277,18 +282,17 @@
         dq_out = sds((n_sub * half, d), f32)
         cost = pl.CostEstimate(flops=2 * 10 ** 9, bytes_accessed=10 ** 7, transcendentals=10 ** 6)
 
-        def attend(bits, k, v, dq=None, finish=False):
+        def attend(bits, k, v, dq=None):
             ins = [first, q2, do2, lse2, delta, start, k, v] + ([dq] if dq is not None else [])
-            outs = (dq_out, dq_out, kv_out, kv_out) if finish else (acc, kv_out, kv_out)
             return pl.pallas_call(
-                functools.partial(attn_kernel, owner_bits=bits, has_dq=dq is not None, finish=finish, scale=scale, **dims),
-                out_shape=outs, in_specs=[sm] + [vm] * (len(ins) - 1), out_specs=(vm,) * len(outs),
-                scratch_shapes=([VMEM((n_sub, d, 2 * half), f32)] if finish else []) + items,
+                functools.partial(attn_kernel, owner_bits=bits, has_dq=dq is not None, scale=scale, **dims),
+                out_shape=(acc, kv_out, kv_out), in_specs=[sm] + [vm] * (len(ins) - 1), out_specs=(vm,) * 3,
+                scratch_shapes=items,
                 compiler_params=pltpu.CompilerParams(vmem_limit_bytes=28 * 2 ** 20),
                 cost_estimate=cost, name='attn_bwd')(*ins)
 
-        def run(bits, k, v, dq=None, finish=False):
-            return attend(bits, k, v, dq, finish)
+        def run(bits, k, v, dq=None):
+            return attend(bits, k, v, dq)
 
         dq, dk_d, dv_d = run((2, 4), kd, vd)
         got_ky = swap(dk_d, 2)
@@ -297,9 +301,12 @@
         got_ko = swap(dk_x, 2)
         dq, dk_y, dv_y = run((4,), ky, vy, dq)
         got_vo = swap(dv_y, 4)
-        dq_own, dq_other, dk_o, dv_o = run((), k_own, v_own, dq, finish=True)
         last_k = swap(dk_y + got_ky, 4)
         last_v = swap(dv_x + got_vx, 2)
+        dq, dk_o, dv_o = run((), k_own, v_own, dq)
+        dq_own, dq_other = pl.pallas_call(
+            split_kernel, out_shape=(dq_out, dq_out), in_specs=[vm], out_specs=(vm, vm),
+            compiler_params=pltpu.CompilerParams(vmem_limit_bytes=28 * 2 ** 20), name='split_dq')(dq)
         got_dq = swap(dq_other, 1)
         d_query = ((dq_own + got_dq) * scale).astype(bf16)
         d_key = (dk_o + got_ko + last_k) * scale

time: 119 us -> 109 us (0.916)
  local copies, waits for them, and re-layouts: 7.2 us -> 0.01 us
  Pallas kernels: 56.4 us -> 53.9 us
    unnamed x18 -> x4, local copies, waits for them, and re-layouts: 7.2 us -> 0.01 us
    pallas_call x4, Pallas kernels: 33 us -> 27.1 us  [attend(): pl.pallas_call(functools.partial(attn_kernel, owner_bits=bits, has_dq=dq...]
    pallas_call x0 -> x1, Pallas kernels: none -> 3.23 us  [local_backward(): pl.pallas_call(split_kernel, out_shape=(dq_out, dq_out), in_specs=[vm], o...]
where the time goes in v1:
time: 109 us
  Pallas kernels  53.9 us (49%)
  waiting for transfers between devices  35.3 us (32%)
  starting transfers between devices  16.1 us (15%)
  other arithmetic  3.18 us (3%)
    ppermute x7, waiting for transfers between devices, swap(): return lax.ppermute(x, 'cp', [(i, i ^ bits) for i in range(cp)])  35.3 us
    pallas_call x4, Pallas kernels, attend(): pl.pallas_call(functools.partial(attn_kernel, owner_bits=bits, has_dq=dq...  27.1 us
    pallas_call x1, Pallas kernels, local_backward(): pl.pallas_call(functools.partial(gather_kernel, **dims), out_shape=tuple(...  23.6 us
    ppermute x7, starting transfers between devices, swap(): return lax.ppermute(x, 'cp', [(i, i ^ bits) for i in range(cp)])  16.1 us
    pallas_call x1, Pallas kernels, local_backward(): pl.pallas_call(split_kernel, out_shape=(dq_out, dq_out), in_specs=[vm], o...  3.23 us
  transfers between devices with their start and end apart: 7, of which 3 were waited for; matrix products, arithmetic and copies ran while one was open for 2% of the time, Pallas kernels for 24%

profile of v1, /device:TPU:0, one launch (start us, length us, event | category | flops | bytes accessed | tf_op | source)
XLA Modules:
  0.0 109.3 jit_solution(8146030421488964141)
XLA Ops:
  0.6 23.6 %gather_kv.1 = (bf16[1088,128]{1,0:T(8,128)(2,1)S(1)}, bf16[1088,128]{1,0:T(8,128)(2,1)S(1)}, bf16[1088,128]{1,0:T(8,128)(2,1)S(1)}, bf16[1088,128]{1,0:T(8,128)...) custom-call(bf16[1088,128]{1,0:T(8,128)(2,1)} %bitcast.14, ...), custom_call_target="tpu_custom_call" | custom-call | tf_op jit(solution)/shard_map/gather_kv/pallas_call | solution.py:265
  24.3 4.1 %attn_bwd.4 = (f32[32,128,256]{2,1,0:T(8,128)S(1)}, f32[1088,128]{1,0:T(8,128)S(1)}, f32[1088,128]{1,0:T(8,128)S(1)}) custom-call(s32[8,32]{1,0:T(8,128)S(1)} %get-tuple-element.29.refs_0_, bf16[2,4096,128]{2,1,0:T(8,128)(2,1)S(1)} %get-tuple-element.30.refs_1_, bf16[2,4096,128]{2,1,0:T(8,128)(2,1)S(1)} %get-tuple-element.31.refs_2_, ...), custom_call_target="tpu_custom_call" | custom-call | flops 2000000000 | bytes 10000000 | tf_op jit(solution)/shard_map/attn_bwd/pallas_call | solution.py:287
  28.3 2.9 %collective-permute-start.5 = (f32[1088,128]{1,0:T(8,128)S(1)}, f32[1088,128]{1,0:T(8,128)S(1)}, u32[]{:S(2)}, u32[]{:S(2)}) collective-permute-start(f32[1088,128]{1,0:T(8,128)S(1)} %get-tuple-element.54), channel_id=1, source_target_pairs={{0,4},{1,5},{2,6},{3,7},{4,0},{5,1},{6,2},{7,3}} | collective-permute-start | bytes 1671176 | tf_op jit(solution)/shard_map/ppermute | solution.py:247
  31.3 5.0 %attn_bwd.5 = (f32[32,128,256]{2,1,0:T(8,128)S(1)}, f32[1088,128]{1,0:T(8,128)S(1)}, f32[1088,128]{1,0:T(8,128)S(1)}) custom-call(s32[8,32]{1,0:T(8,128)S(1)} %get-tuple-element.29.refs_0_, bf16[2,4096,128]{2,1,0:T(8,128)(2,1)S(1)} %get-tuple-element.30.refs_1_, bf16[2,4096,128]{2,1,0:T(8,128)(2,1)S(1)} %get-tuple-element.31.refs_2_, ...), custom_call_target="tpu_custom_call" | custom-call | flops 2000000000 | bytes 10000000 | tf_op jit(solution)/shard_map/attn_bwd/pallas_call | solution.py:287
  36.3 0.0 copy-start
  36.3 0.0 copy-start.1
  36.3 11.0 %attn_bwd.6 = (f32[32,128,256]{2,1,0:T(8,128)S(1)}, f32[1088,128]{1,0:T(8,128)S(1)}, f32[1088,128]{1,0:T(8,128)S(1)}) custom-call(s32[8,32]{1,0:T(8,128)S(1)} %get-tuple-element.29.refs_0_, bf16[2,4096,128]{2,1,0:T(8,128)(2,1)S(1)} %get-tuple-element.30.refs_1_, bf16[2,4096,128]{2,1,0:T(8,128)(2,1)S(1)} %get-tuple-element.31.refs_2_, ...), custom_call_target="tpu_custom_call" | custom-call | flops 2000000000 | bytes 10000000 | tf_op jit(solution)/shard_map/attn_bwd/pallas_call | solution.py:287
  47.2 0.0 copy-done
  47.3 0.0 copy-done.1
  47.3 7.1 %attn_bwd.7 = (f32[32,128,256]{2,1,0:T(8,128)S(1)}, f32[1088,128]{1,0:T(8,128)S(1)}, f32[1088,128]{1,0:T(8,128)S(1)}) custom-call(s32[8,32]{1,0:T(8,128)S(1)} %get-tuple-element.29.refs_0_, bf16[2,4096,128]{2,1,0:T(8,128)(2,1)S(1)} %get-tuple-element.30.refs_1_, bf16[2,4096,128]{2,1,0:T(8,128)(2,1)S(1)} %get-tuple-element.31.refs_2_, ...), custom_call_target="tpu_custom_call" | custom-call | flops 2000000000 | bytes 10000000 | tf_op jit(solution)/shard_map/attn_bwd/pallas_call | solution.py:287
  54.3 3.2 %split_dq.1 = (f32[4096,128]{1,0:T(8,128)S(1)}, f32[4096,128]{1,0:T(8,128)S(1)}) custom-call(f32[32,128,256]{2,1,0:T(8,128)S(1)} %get-tuple-element.44.dq_ref), custom_call_target="tpu_custom_call" | custom-call | tf_op jit(solution)/shard_map/split_dq/pallas_call | solution.py:307
  57.6 11.1 %collective-permute-start = (f32[4096,128]{1,0:T(8,128)S(1)}, f32[4096,128]{1,0:T(8,128)S(1)}, u32[]{:S(2)}, u32[]{:S(2)}) collective-permute-start(f32[4096,128]{1,0:T(8,128)S(1)} %get-tuple-element.46), channel_id=1, source_target_pairs={{0,1},{1,0},{2,3},{3,2},{4,5},{5,4},{6,7},{7,6}} | collective-permute-start | bytes 6291464 | tf_op jit(solution)/shard_map/ppermute | solution.py:247
  68.7 0.0 collective-permute-start.2
  68.7 0.0 collective-permute-start.4
  68.7 0.0 collective-permute-done.5
  68.7 0.1 add.26
  68.7 2.0 %collective-permute-start.6 = (f32[1088,128]{1,0:T(8,128)S(1)}, f32[1088,128]{1,0:T(8,128)S(1)}, u32[]{:S(2)}, u32[]{:S(2)}) collective-permute-start(f32[1088,128]{1,0:T(8,128)S(1)} %add.26), channel_id=1, source_target_pairs={{0,2},{1,3},{2,0},{3,1},{4,6},{5,7},{6,4},{7,5}} | collective-permute-start | bytes 1671176 | tf_op jit(solution)/shard_map/ppermute | solution.py:247
  70.8 0.0 collective-permute-start.1
  70.8 13.3 %collective-permute-done.2 = f32[1088,128]{1,0:T(8,128)S(1)} collective-permute-done((f32[1088,128]{1,0:T(8,128)S(1)}, f32[1088,128]{1,0:T(8,128)S(1)}, u32[]{:S(2)}, u32[]{:S(2)}) %collective-permute-start.2) | collective-permute-done | bytes 557088 | tf_op jit(solution)/shard_map/ppermute | solution.py:247
  84.2 0.1 add.23
  84.2 0.0 collective-permute-start.3
  84.2 0.0 collective-permute-done.4
  84.3 11.8 %collective-permute-done.6 = f32[1088,128]{1,0:T(8,128)S(1)} collective-permute-done((f32[1088,128]{1,0:T(8,128)S(1)}, f32[1088,128]{1,0:T(8,128)S(1)}, u32[]{:S(2)}, u32[]{:S(2)}) %collective-permute-start.6) | collective-permute-done | bytes 557088 | tf_op jit(solution)/shard_map/ppermute | solution.py:247
  96.1 0.9 add_add_fusion
  97.0 10.1 %collective-permute-done.1 = f32[1088,128]{1,0:T(8,128)S(1)} collective-permute-done((f32[1088,128]{1,0:T(8,128)S(1)}, f32[1088,128]{1,0:T(8,128)S(1)}, u32[]{:S(2)}, u32[]{:S(2)}) %collective-permute-start.1) | collective-permute-done | bytes 557088 | tf_op jit(solution)/shard_map/ppermute | solution.py:247
  107.1 0.0 collective-permute-done.3
  107.1 0.9 add_multiply_fusion
  108.0 0.0 collective-permute-done
  108.0 1.2 %multiply_convert_fusion = bf16[4096,128]{1,0:T(8,128)(2,1)} fusion(f32[4096,128]{1,0:T(8,128)S(1)} %get-tuple-element.45, f32[4096,128]{1,0:T(8,128)S(1)} %collective-permute-done), kind=kLoop, calls=%fused_computation | loop fusion | flops 1572864 | bytes 5242880 | tf_op jit(solution)/shard_map/convert_element_type | solution.py:311
Async XLA Ops:
  28.3 40.3 %collective-permute-start.5 = (f32[1088,128]{1,0:T(8,128)S(1)}, f32[1088,128]{1,0:T(8,128)S(1)}, u32[]{:S(2)}, u32[]{:S(2)}) collective-permute-start(f32[1088,128]{1,0:T(8,128)S(1)} %get-tuple-element.54), channel_id=1, source_target_pairs={{0,4},{1,5},{2,6},{3,7},{4,0},{5,1},{6,2},{7,3}} | collective-permute-start | bytes 1671176 | tf_op jit(solution)/shard_map/ppermute | solution.py:247
  36.3 11.0 %copy-start = (bf16[1088,1,128]{2,0,1:T(8,128)(2,1)S(1)}, bf16[1088,1,128]{2,0,1:T(8,128)(2,1)}, u32[]{:S(2)}) copy-start(bf16[1088,1,128]{2,0,1:T(8,128)(2,1)} %param.11) | copy-start | bytes 835588
  36.3 11.0 %copy-start.1 = (bf16[1088,1,128]{2,0,1:T(8,128)(2,1)S(1)}, bf16[1088,1,128]{2,0,1:T(8,128)(2,1)}, u32[]{:S(2)}) copy-start(bf16[1088,1,128]{2,0,1:T(8,128)(2,1)} %param.12) | copy-start | bytes 835588
  57.6 50.5 %collective-permute-start = (f32[4096,128]{1,0:T(8,128)S(1)}, f32[4096,128]{1,0:T(8,128)S(1)}, u32[]{:S(2)}, u32[]{:S(2)}) collective-permute-start(f32[4096,128]{1,0:T(8,128)S(1)} %get-tuple-element.46), channel_id=1, source_target_pairs={{0,1},{1,0},{2,3},{3,2},{4,5},{5,4},{6,7},{7,6}} | collective-permute-start | bytes 6291464 | tf_op jit(solution)/shard_map/ppermute | solution.py:247
  68.7 15.5 %collective-permute-start.2 = (f32[1088,128]{1,0:T(8,128)S(1)}, f32[1088,128]{1,0:T(8,128)S(1)}, u32[]{:S(2)}, u32[]{:S(2)}) collective-permute-start(f32[1088,128]{1,0:T(8,128)S(1)} %get-tuple-element.50), channel_id=1, source_target_pairs={{0,2},{1,3},{2,0},{3,1},{4,6},{5,7},{6,4},{7,5}} | collective-permute-start | bytes 1671176 | tf_op jit(solution)/shard_map/ppermute | solution.py:247
  68.7 15.6 %collective-permute-start.4 = (f32[1088,128]{1,0:T(8,128)S(1)}, f32[1088,128]{1,0:T(8,128)S(1)}, u32[]{:S(2)}, u32[]{:S(2)}) collective-permute-start(f32[1088,128]{1,0:T(8,128)S(1)} %get-tuple-element.52), channel_id=1, source_target_pairs={{0,4},{1,5},{2,6},{3,7},{4,0},{5,1},{6,2},{7,3}} | collective-permute-start | bytes 1671176 | tf_op jit(solution)/shard_map/ppermute | solution.py:247
  68.7 27.4 %collective-permute-start.6 = (f32[1088,128]{1,0:T(8,128)S(1)}, f32[1088,128]{1,0:T(8,128)S(1)}, u32[]{:S(2)}, u32[]{:S(2)}) collective-permute-start(f32[1088,128]{1,0:T(8,128)S(1)} %add.26), channel_id=1, source_target_pairs={{0,2},{1,3},{2,0},{3,1},{4,6},{5,7},{6,4},{7,5}} | collective-permute-start | bytes 1671176 | tf_op jit(solution)/shard_map/ppermute | solution.py:247
  70.8 36.3 %collective-permute-start.1 = (f32[1088,128]{1,0:T(8,128)S(1)}, f32[1088,128]{1,0:T(8,128)S(1)}, u32[]{:S(2)}, u32[]{:S(2)}) collective-permute-start(f32[1088,128]{1,0:T(8,128)S(1)} %get-tuple-element.48), channel_id=1, source_target_pairs={{0,2},{1,3},{2,0},{3,1},{4,6},{5,7},{6,4},{7,5}} | collective-permute-start | bytes 1671176 | tf_op jit(solution)/shard_map/ppermute | solution.py:247
  84.2 22.9 %collective-permute-start.3 = (f32[1088,128]{1,0:T(8,128)S(1)}, f32[1088,128]{1,0:T(8,128)S(1)}, u32[]{:S(2)}, u32[]{:S(2)}) collective-permute-start(f32[1088,128]{1,0:T(8,128)S(1)} %add.23), channel_id=1, source_target_pairs={{0,4},{1,5},{2,6},{3,7},{4,0},{5,1},{6,2},{7,3}} | collective-permute-start | bytes 1671176 | tf_op jit(solution)/shard_map/ppermute | solution.py:247

commit v2 on v1

v2 whole, which is shorter than its diff:
```python
import functools

import jax
import jax.numpy as jnp
from jax import lax
from jax.experimental import pallas as pl
from jax.experimental.pallas import tpu as pltpu
from jax.sharding import PartitionSpec as P


LOG2E = 1.4426950408889634
NT = (((1,), (1,)), ((), ()))
MESH = pl.DeviceIdType.MESH
VMEM, SMEM = pltpu.VMEM, pltpu.SMEM
HIGHEST = lax.Precision.HIGHEST
KT = 256
UNROLL = 4


def flip(me, bit):
    return me + bit - 2 * bit * lax.rem(me // bit, 2)


def prep_kernel(k_ref, v_ref, q_ref, do_ref, o_ref, lse_ref, ids_ref,
                kx_ref, vx_ref, ky_ref, vy_ref, q2_ref, do2_ref, lse2_ref, delta_ref, start_ref, first_ref,
                o2_ref, lraw_ref, mark_ref, send_sem, recv_sem, load_sem, *, pre, sub_len, loc, heads):
    me = lax.axis_index('cp')
    core = lax.rem(me, 2)
    nx, ny, partner = flip(me, 2), flip(me, 4), flip(me, 1)
    barrier = pltpu.get_barrier_semaphore()
    for other in (nx, ny, partner):
        pl.semaphore_signal(barrier, inc=1, device_id={'cp': other}, device_id_type=MESH)
    pl.semaphore_wait(barrier, 3)
    pairs = [(do_ref, do2_ref), (o_ref, o2_ref), (lse_ref, lraw_ref), (q_ref, q2_ref)]
    moves = [(s, r.at[core], partner) for s, r in pairs]
    moves += [(k_ref, kx_ref, nx), (v_ref, vy_ref, ny), (v_ref, vx_ref, nx), (k_ref, ky_ref, ny)]
    sends = [pltpu.make_async_remote_copy(src_ref=s, dst_ref=r, send_sem=send_sem.at[i], recv_sem=recv_sem.at[i],
                                          device_id={'cp': to}, device_id_type=MESH) for i, (s, r, to) in enumerate(moves)]
    loads = [pltpu.make_async_copy(s, r.at[core], load_sem.at[i]) for i, (s, r) in enumerate(pairs)]
    for copy in sends[4:] + sends[:4] + loads:
        copy.start()

    n_rows = ids_ref.shape[0]
    n_sub = lraw_ref.shape[1]
    pad = mark_ref.shape[0]
    load_ids = pltpu.make_async_copy(ids_ref, mark_ref.at[pl.ds(0, n_rows)], load_sem.at[4])
    load_ids.start()
    mark_ref[pl.ds(n_rows, pad - n_rows), :] = jnp.zeros((pad - n_rows, 128), jnp.int32)
    load_ids.wait()
    ids = mark_ref[...]
    lane = lax.broadcasted_iota(jnp.int32, (pad, 128), 1)
    row = lax.broadcasted_iota(jnp.int32, (pad, 128), 0)
    prev = pltpu.roll(ids, 1, axis=1)
    prev = jnp.where(lane == 0, pltpu.roll(prev, 1, axis=0), prev)
    acc = jnp.where(ids != prev, row * 128 + lane, 0)
    for sh in (1, 2, 4, 8, 16, 32, 64):
        acc = jnp.maximum(acc, jnp.where(lane >= sh, pltpu.roll(acc, sh, axis=1), 0))
    carry = jnp.max(acc, axis=1, keepdims=True) + jnp.zeros((pad, 128), jnp.int32)
    carry = jnp.where(row >= 1, pltpu.roll(carry, 1, axis=0), 0)
    sh = 1
    while sh < pad:
        carry = jnp.maximum(carry, jnp.where(row >= sh, pltpu.roll(carry, sh, axis=0), 0))
        sh *= 2
    starts = jnp.maximum(acc, carry).astype(jnp.float32)

    def hdot(a, b, dims=None):
        dims = (((1,), (0,)), ((), ())) if dims is None else dims
        return lax.dot_general(a, b, dims, precision=HIGHEST, preferred_element_type=jnp.float32)

    per = sub_len // 128
    off = (me // 2) * 2 * loc
    r_sub = lax.broadcasted_iota(jnp.int32, (n_sub, pad), 0)
    r_row = lax.broadcasted_iota(jnp.int32, (n_sub, pad), 1)
    pick = jnp.where(r_row == pre // 128 + per * r_sub + off // 128, 1.0, 0.0)
    sub_starts = hdot(pick, starts)
    src = lax.broadcasted_iota(jnp.int32, (128, 128), 0)
    dst = lax.broadcasted_iota(jnp.int32, (128, 128), 1)
    for e in range(2):
        spread = jnp.where(src == lax.rem(off, 128) + e * loc + dst // heads, 1.0, 0.0)
        rows_start = hdot(sub_starts, spread)
        start_ref[e] = rows_start.astype(jnp.int32)
        if e == 0:
            head = jnp.where(lax.broadcasted_iota(jnp.int32, (8, 128), 1) == 0, 1.0, 0.0)
            first_ref[...] = hdot(head, rows_start, NT).astype(jnp.int32)

    def delta_of(e, o_part):
        def body(t, c):
            r0 = pl.multiple_of(t * 128, 128)
            prod = do2_ref[e, pl.ds(r0, 128), :].astype(jnp.float32) * o_part[pl.ds(r0, 128), :].astype(jnp.float32)
            delta_ref[e, pl.ds(t, 1), :] = jnp.sum(prod.T, axis=0, keepdims=True)
            return c

        lax.fori_loop(0, n_sub, body, 0)

    for load in loads:
        load.wait()
    delta_of(core, o2_ref.at[core])
    for copy in sends[:3]:
        copy.wait_recv()
    delta_of(1 - core, o2_ref.at[1 - core])
    tok = lax.broadcasted_iota(jnp.int32, (loc, 128), 0)
    tok_lane = lax.broadcasted_iota(jnp.int32, (loc, 128), 1)
    tok_spread = jnp.where(tok == tok_lane // heads, 1.0, 0.0)
    head_of = lax.broadcasted_iota(jnp.int32, (n_sub * heads, 128), 0)
    head_lane = lax.broadcasted_iota(jnp.int32, (n_sub * heads, 128), 1)
    own_head = lax.rem(head_of, heads) == lax.rem(head_lane, heads)
    g_sub = lax.broadcasted_iota(jnp.int32, (n_sub, n_sub * heads), 0)
    g_row = lax.broadcasted_iota(jnp.int32, (n_sub, n_sub * heads), 1)
    group = jnp.where(g_row // heads == g_sub, 1.0, 0.0)
    for e in range(2):
        wide = hdot(lraw_ref[e].reshape(n_sub * heads, loc), tok_spread)
        lse2_ref[e] = hdot(group, jnp.where(own_head, wide, 0.0)) * LOG2E
    for copy in sends[3:]:
        copy.wait_recv()
    for copy in sends:
        copy.wait_send()


def split_kernel(dq_ref, own_ref, other_ref):
    n_sub, _, rows = dq_ref.shape
    half = rows // 2
    core = lax.rem(lax.axis_index('cp'), 2)
    mine = pl.multiple_of(core * half, half)
    theirs = pl.multiple_of((1 - core) * half, half)

    def put(t, c):
        r0 = pl.multiple_of(t * half, half)
        other_ref[pl.ds(r0, half), :] = dq_ref[t, :, pl.ds(theirs, half)].T
        own_ref[pl.ds(r0, half), :] = dq_ref[t, :, pl.ds(mine, half)].T
        return c

    lax.fori_loop(0, n_sub, put, 0)


def attn_kernel(*refs, blocks, row0, n_keys, outs, has_dq, scale, blk, pre, sub_len, loc, heads):
    first_ref, q_ref, do_ref, lse_ref, delta_ref, start_ref = refs[:6]
    nb = len(blocks)
    k_in, v_in, refs = refs[6:6 + nb], refs[6 + nb:6 + 2 * nb], refs[6 + 2 * nb:]
    if has_dq:
        dq_in, refs = refs[0], refs[1:]
    dq_ref, grad_out, refs = refs[0], refs[1:1 + len(outs)], refs[1 + len(outs):]
    it_t, it_k, it_lo, it_base, p_ref, ds_ref, kpos_ref, k_ref, v_ref, dk_ref, dv_ref = refs
    me = lax.axis_index('cp')
    n_sub, half = lse_ref.shape[1], lse_ref.shape[2]
    rows = 2 * half
    pos0 = pre + (me // 2) * 2 * loc
    for b in range(nb):
        k_ref[b * n_keys:(b + 1) * n_keys, :] = k_in[b][row0:row0 + n_keys, :]
        v_ref[b * n_keys:(b + 1) * n_keys, :] = v_in[b][row0:row0 + n_keys, :]
    dk_ref[...] = jnp.zeros_like(dk_ref)
    dv_ref[...] = jnp.zeros_like(dv_ref)
    if has_dq:
        dq_ref[...] = dq_in[...]
    else:
        dq_ref[...] = jnp.zeros_like(dq_ref)

    n_items = 0
    for b, bits in enumerate(blocks):
        owner = me
        for bit in bits:
            owner = flip(owner, bit)
        blo = owner * blk + row0

        def more(c, blo=blo):
            return (c[0] < n_sub) & (first_ref[0, jnp.minimum(c[0], n_sub - 1)] < blo + n_keys)

        def add_tile(c, b=b, blo=blo):
            t, n = c
            lo = jnp.maximum(first_ref[0, t], blo)
            hi = jnp.minimum(pos0 + t * sub_len + 2 * loc - 1, blo + n_keys - 1)
            off = (lo - blo) // 16 * 16
            cnt = (hi - blo - off) // KT + 1

            def add_item(i, m):
                it_t[m] = t
                it_k[m] = b * n_keys + jnp.minimum(off + i * KT, n_keys - KT)
                it_lo[m] = blo + off + i * KT
                it_base[m] = blo - b * n_keys
                return m + 1

            return t + 1, lax.fori_loop(0, cnt, add_item, n)

        t_first = jnp.maximum(blo - pos0 - 2 * loc + sub_len, 0) // sub_len
        n_items = lax.while_loop(more, add_tile, (t_first, n_items))[1]
    for u in range(UNROLL - 1):
        it_t[n_items + u] = 0
        it_k[n_items + u] = 0
        it_lo[n_items + u] = 1 << 30
        it_base[n_items + u] = 0

    def two(ref, t):
        return jnp.concatenate([ref[0, pl.ds(t, 1), :], ref[1, pl.ds(t, 1), :]], axis=1)

    lane = lax.broadcasted_iota(jnp.int32, (1, rows), 1)
    zero = jnp.zeros((16, rows), jnp.bfloat16)
    kpos_ref[...] = lax.broadcasted_iota(jnp.int32, (KT, rows), 0).astype(jnp.float32).astype(jnp.bfloat16)

    def item(w, u):
        m = w * UNROLL + u
        t = it_t[m]
        k0 = pl.multiple_of(it_k[m], 16)
        r0 = pl.multiple_of(t * half, half)
        q = jnp.concatenate([q_ref[0, pl.ds(r0, half), :], q_ref[1, pl.ds(r0, half), :]], axis=0)
        do = jnp.concatenate([do_ref[0, pl.ds(r0, half), :], do_ref[1, pl.ds(r0, half), :]], axis=0)
        return m, t, k0, q, do

    def scores(w):
        out = []
        for u in range(UNROLL):
            m, t, k0, q, do = item(w, u)
            s = lax.dot_general(k_ref[pl.ds(k0, KT), :], q, NT, preferred_element_type=jnp.float32)
            dp = lax.dot_general(v_ref[pl.ds(k0, KT), :], do, NT, preferred_element_type=jnp.float32)
            lo = jnp.maximum(two(start_ref, t), it_lo[m]) - (k0 + it_base[m])
            qpos = lane // heads + (pos0 + t * sub_len - k0 - it_base[m])
            lo = packed(jnp.clip(lo, 0, KT))
            qpos = packed(jnp.clip(qpos, -1, KT))
            out.append((s, dp, lo, qpos, two(lse_ref, t), two(delta_ref, t)))
        return out

    def packed(x):
        return jnp.broadcast_to(x.astype(jnp.float32), (16, rows)).astype(jnp.bfloat16)

    def probs(parts):
        for u in range(UNROLL):
            s, dp, lo, qpos, lse, delta = parts[u]
            for g in range(KT // 16):
                r = slice(16 * g, 16 * g + 16)
                kpos = kpos_ref[r, :]
                allowed = (kpos >= lo) & (kpos <= qpos)
                p = jnp.exp2(s[r, :] * (scale * LOG2E) - lse)
                ds = p * (dp[r, :] - delta)
                p_ref[u, r, :] = jnp.where(allowed, p.astype(jnp.bfloat16), zero)
                ds_ref[u, r, :] = jnp.where(allowed, ds.astype(jnp.bfloat16), zero)

    def grads(w):
        for u in range(UNROLL):
            _, t, k0, q, do = item(w, u)
            p, ds = p_ref[u], ds_ref[u]
            dv_ref[pl.ds(k0, KT), :] += jnp.dot(p, do, preferred_element_type=jnp.float32)
            dk_ref[pl.ds(k0, KT), :] += jnp.dot(ds, q, preferred_element_type=jnp.float32)
            dq_ref[t] += jnp.dot(k_ref[pl.ds(k0, KT), :].T, ds, preferred_element_type=jnp.float32)

    def body(w, c):
        probs(scores(w))
        grads(w)
        return c

    lax.fori_loop(0, (n_items + UNROLL - 1) // UNROLL, body, 0)
    for ref, (kind, which) in zip(grad_out, outs):
        acc = dk_ref if kind == 'k' else dv_ref
        ref[...] = acc[which[0] * n_keys:(which[-1] + 1) * n_keys, :]


def solution(mesh):
    cp = mesh.shape['cp']
    q_spec = P(None, 'cp', 'tp', None)
    lse_spec = P(None, 'cp', 'tp')
    kv_spec = P('cp', 'tp', None)

    def swap(x, bits):
        return lax.ppermute(x, 'cp', [(i, i ^ bits) for i in range(cp)])

    def local_backward(query, out_act, out_grad, row_lse, key_act, value_act, doc_ids):
        n_sub, loc, heads, d = query.shape
        blk = key_act.shape[0]
        n_keys = blk * cp
        half = loc * heads
        sub_len = loc * cp
        pre = n_keys - n_sub * sub_len
        scale = d ** -0.5
        f32, bf16, i32 = jnp.float32, jnp.bfloat16, jnp.int32
        dims = dict(pre=pre, sub_len=sub_len, loc=loc, heads=heads)
        vm = pl.BlockSpec(memory_space=VMEM)
        sm = pl.BlockSpec(memory_space=SMEM)
        hbm = pl.BlockSpec(memory_space=pltpu.HBM)
        sds = jax.ShapeDtypeStruct
        k_own, v_own = key_act.reshape(blk, d), value_act.reshape(blk, d)
        pad = (n_keys // 128 + 7) // 8 * 8
        acc = sds((n_sub, d, 2 * half), f32)
        dq_out = sds((n_sub * half, d), f32)
        cost = pl.CostEstimate(flops=2 * 10 ** 9, bytes_accessed=10 ** 7, transcendentals=10 ** 6)

        def attend(keys, values, dq, blocks, row0, n_rows, outs):
            nb = len(blocks)
            ins = [first, q2, do2, lse2, delta, start, *keys, *values] + ([dq] if dq is not None else [])
            cap = nb * n_sub * (-(-n_rows // KT) + 1) + UNROLL
            kv = (nb * n_rows, d)
            return pl.pallas_call(
                functools.partial(attn_kernel, blocks=blocks, row0=row0, n_keys=n_rows, outs=outs, has_dq=dq is not None,
                                  scale=scale, blk=blk, **dims),
                out_shape=(acc,) + tuple(sds((len(w) * n_rows, d), f32) for _, w in outs),
                in_specs=[sm] + [vm] * (len(ins) - 1), out_specs=(vm,) * (1 + len(outs)),
                scratch_shapes=[SMEM((cap,), i32)] * 4 + [VMEM((UNROLL, KT, 2 * half), bf16)] * 2 + [VMEM((KT, 2 * half), bf16)]
                + [VMEM(kv, bf16)] * 2 + [VMEM(kv, f32)] * 2,
                compiler_params=pltpu.CompilerParams(vmem_limit_bytes=28 * 2 ** 20),
                cost_estimate=cost, name='attn_bwd')(*ins)

        kx, vx, ky, vy, q2, do2, lse2, delta, start, first = pl.pallas_call(
            functools.partial(prep_kernel, **dims),
            out_shape=tuple([sds((blk, d), bf16)] * 4 + [sds((2, n_sub * half, d), bf16)] * 2 + [sds((2, n_sub, half), f32)] * 2
                            + [sds((2, n_sub, half), i32), sds((8, n_sub), i32)]),
            in_specs=[hbm] * 7, out_specs=(vm,) * 10,
            scratch_shapes=[VMEM((2, n_sub * half, d), bf16), VMEM((2, n_sub, heads, loc), f32), VMEM((pad, 128), i32),
                            pltpu.SemaphoreType.DMA((8,)), pltpu.SemaphoreType.DMA((8,)), pltpu.SemaphoreType.DMA((5,))],
            compiler_params=pltpu.CompilerParams(collective_id=0, has_side_effects=True, vmem_limit_bytes=24 * 2 ** 20),
            name='prep',
        )(*[pltpu.with_memory_space_constraint(x, pltpu.HBM) for x in (
            k_own, v_own, query.reshape(-1, d), out_grad.reshape(-1, d), out_act.reshape(-1, d),
            row_lse.transpose(0, 2, 1), doc_ids.reshape(n_keys // 128, 128))])
        kd = swap(kx, 4)
        vd = swap(vy, 2)
        both = (('k', (0,)), ('v', (0,)))
        four = (('k', (0,)), ('k', (1,)), ('v', (0,)), ('v', (1,)))
        dq, dk_x, dk_y, dv_x, dv_y = attend([kx, ky], [vx, vy], None, ((2,), (4,)), 0, blk, four)
        got_ko = swap(dk_x, 2)
        got_vo = swap(dv_y, 4)
        dq, dk_d, dv_d = attend([kd], [vd], dq, ((2, 4),), 0, blk, both)
        got_ky = swap(dk_d, 2)
        got_vx = swap(dv_d, 4)
        dq, dk_o, dv_o = attend([k_own], [v_own], dq, ((),), 0, blk, both)
        last_k = swap(dk_y + got_ky, 4)
        last_v = swap(dv_x + got_vx, 2)
        dq_own, dq_other = pl.pallas_call(
            split_kernel, out_shape=(dq_out, dq_out), in_specs=[vm], out_specs=(vm, vm),
            compiler_params=pltpu.CompilerParams(vmem_limit_bytes=28 * 2 ** 20), name='split_dq')(dq)
        got_dq = swap(dq_other, 1)
        d_query = ((dq_own + got_dq) * scale).astype(bf16)
        d_key = (dk_o + got_ko + last_k) * scale
        d_value = dv_o + got_vo + last_v
        return d_query.reshape(query.shape), d_key.reshape(key_act.shape), d_value.reshape(value_act.shape)

    return jax.shard_map(local_backward, mesh=mesh, in_specs=(q_spec, q_spec, q_spec, lse_spec, kv_spec, kv_spec, P()), out_specs=(q_spec, kv_spec, kv_spec), check_vma=False)
```

time: 109 us -> 101 us (0.927)
  Pallas kernels: 53.9 us -> 46.5 us
  waiting for transfers between devices: 35.3 us -> 33.6 us
    pallas_call x5 -> x4, Pallas kernels: 50.7 us -> 43.3 us  [the longest x3 25.6 us: attend(): pl.pallas_call(functools.partial(attn_kernel, blocks=blocks, row0=row0, n...]
    ppermute x7 -> x9, waiting for transfers between devices: 35.3 us -> 33.6 us  [swap(): return lax.ppermute(x, 'cp', [(i, i ^ bits) for i in range(cp)])]
    ppermute x7 -> x9, starting transfers between devices: 16.1 us -> 16.4 us  [swap(): return lax.ppermute(x, 'cp', [(i, i ^ bits) for i in range(cp)])]
  transfers between devices with their start and end apart: 7 -> 9, of which waited for: 3 -> 4; matrix products, arithmetic and copies ran while one was open for 2% -> 2% of each run, Pallas kernels for 24% -> 25%
where the time goes in v2:
time: 101 us; the launch traced here: 100 us
  Pallas kernels  46.5 us (46%)
  waiting for transfers between devices  33.6 us (33%)
  starting transfers between devices  16.4 us (16%)
  other arithmetic  3.14 us (3%)
    ppermute x9, waiting for transfers between devices, swap(): return lax.ppermute(x, 'cp', [(i, i ^ bits) for i in range(cp)])  33.6 us
    pallas_call x3, Pallas kernels, attend(): pl.pallas_call(functools.partial(attn_kernel, blocks=blocks, row0=row0, n...  25.6 us
    pallas_call x1, Pallas kernels, local_backward(): pl.pallas_call(functools.partial(prep_kernel, **dims), out_shape=tuple([s...  17.6 us
    ppermute x9, starting transfers between devices, swap(): return lax.ppermute(x, 'cp', [(i, i ^ bits) for i in range(cp)])  16.4 us
    pallas_call x1, Pallas kernels, local_backward(): pl.pallas_call(split_kernel, out_shape=(dq_out, dq_out), in_specs=[vm], o...  3.23 us
  transfers between devices with their start and end apart: 9, of which 4 were waited for; matrix products, arithmetic and copies ran while one was open for 2% of the time, Pallas kernels for 25%

profile of v2, /device:TPU:0, one launch (start us, length us, event | category | flops | bytes accessed | tf_op | source)
XLA Modules:
  0.0 100.4 jit_solution(14509943636020406094)
XLA Ops:
  0.6 17.6 %prep.1 = (bf16[1088,128]{1,0:T(8,128)(2,1)S(1)}, bf16[1088,128]{1,0:T(8,128)(2,1)S(1)}, bf16[1088,128]{1,0:T(8,128)(2,1)S(1)}, bf16[1088,128]{1,0:T(8,128)(2,1)...) custom-call(bf16[1088,128]{1,0:T(8,128)(2,1)} %bitcast.14, ...), custom_call_target="tpu_custom_call" | custom-call | tf_op jit(solution)/shard_map/prep/pallas_call | solution.py:298
  18.2 1.0 collective-permute-start
  19.2 1.1 %collective-permute-start.1 = (bf16[1088,128]{1,0:T(8,128)(2,1)S(1)}, bf16[1088,128]{1,0:T(8,128)(2,1)S(1)}, u32[]{:S(2)}, u32[]{:S(2)}) collective-permute-start(bf16[1088,128]{1,0:T(8,128)(2,1)S(1)} %get-tuple-element.33.refs_9_), channel_id=1, source_target_pairs={{0,2},{1,3},{2,0},{3,1},{4,6},{5,7},{6,4},{7,5}} | collective-permute-start | bytes 835592 | tf_op jit(solution)/shard_map/ppermute | solution.py:261
  20.3 14.6 %attn_bwd.3 = (f32[32,128,256]{2,1,0:T(8,128)S(1)}, f32[1088,128]{1,0:T(8,128)S(1)}, f32[1088,128]{1,0:T(8,128)S(1)}, f32[1088,128]{1,0:T(8,128)S(1)}, f32[1088,128]{1,0:T(8,128)S(1)}) custom-call(s32[8,32]{1,0:T(8,128)S(1)} %get-tuple-element.26.refs_0_, bf16[2,4096,128]{2,1,0:T(8,128)(2,1)S(1)} %get-tuple-element.27.refs_1_, ...), custom_call_target="tpu_custom_call" | custom-call | flops 2000000000 | bytes 10000000 | tf_op jit(solution)/shard_map/attn_bwd/pallas_call | solution.py:288
  34.9 0.0 collective-permute-done.refs_6_
  34.9 0.0 collective-permute-done.1.refs_7_
  35.0 0.0 copy-start
  35.0 0.0 copy-start.1
  35.0 4.1 %attn_bwd.4 = (f32[32,128,256]{2,1,0:T(8,128)S(1)}, f32[1088,128]{1,0:T(8,128)S(1)}, f32[1088,128]{1,0:T(8,128)S(1)}) custom-call(s32[8,32]{1,0:T(8,128)S(1)} %get-tuple-element.26.refs_0_, bf16[2,4096,128]{2,1,0:T(8,128)(2,1)S(1)} %get-tuple-element.27.refs_1_, bf16[2,4096,128]{2,1,0:T(8,128)(2,1)S(1)} %get-tuple-element.28.refs_2_, ...), custom_call_target="tpu_custom_call" | custom-call | flops 2000000000 | bytes 10000000 | tf_op jit(solution)/shard_map/attn_bwd/pallas_call | solution.py:288
  39.0 0.0 collective-permute-start.7
  39.1 0.0 copy-done
  39.1 0.0 copy-done.1
  39.1 7.0 %attn_bwd.5 = (f32[32,128,256]{2,1,0:T(8,128)S(1)}, f32[1088,128]{1,0:T(8,128)S(1)}, f32[1088,128]{1,0:T(8,128)S(1)}) custom-call(s32[8,32]{1,0:T(8,128)S(1)} %get-tuple-element.26.refs_0_, bf16[2,4096,128]{2,1,0:T(8,128)(2,1)S(1)} %get-tuple-element.27.refs_1_, bf16[2,4096,128]{2,1,0:T(8,128)(2,1)S(1)} %get-tuple-element.28.refs_2_, ...), custom_call_target="tpu_custom_call" | custom-call | flops 2000000000 | bytes 10000000 | tf_op jit(solution)/shard_map/attn_bwd/pallas_call | solution.py:288
  46.1 3.2 %split_dq.1 = (f32[4096,128]{1,0:T(8,128)S(1)}, f32[4096,128]{1,0:T(8,128)S(1)}) custom-call(f32[32,128,256]{2,1,0:T(8,128)S(1)} %get-tuple-element.38.dq_ref), custom_call_target="tpu_custom_call" | custom-call | tf_op jit(solution)/shard_map/split_dq/pallas_call | solution.py:323
  49.3 8.7 %collective-permute-start.2 = (f32[4096,128]{1,0:T(8,128)S(1)}, f32[4096,128]{1,0:T(8,128)S(1)}, u32[]{:S(2)}, u32[]{:S(2)}) collective-permute-start(f32[4096,128]{1,0:T(8,128)S(1)} %get-tuple-element.40), channel_id=1, source_target_pairs={{0,1},{1,0},{2,3},{3,2},{4,5},{5,4},{6,7},{7,6}} | collective-permute-start | bytes 6291464 | tf_op jit(solution)/shard_map/ppermute | solution.py:261
  58.0 3.6 %collective-permute-start.4 = (f32[1088,128]{1,0:T(8,128)S(1)}, f32[1088,128]{1,0:T(8,128)S(1)}, u32[]{:S(2)}, u32[]{:S(2)}) collective-permute-start(f32[1088,128]{1,0:T(8,128)S(1)} %get-tuple-element.44), channel_id=1, source_target_pairs={{0,2},{1,3},{2,0},{3,1},{4,6},{5,7},{6,4},{7,5}} | collective-permute-start | bytes 1671176 | tf_op jit(solution)/shard_map/ppermute | solution.py:261
  61.6 0.0 collective-permute-start.6
  61.6 0.0 collective-permute-done.7
  61.6 0.1 add.26
  61.6 0.0 collective-permute-start.8
  61.7 2.0 %collective-permute-start.3 = (f32[1088,128]{1,0:T(8,128)S(1)}, f32[1088,128]{1,0:T(8,128)S(1)}, u32[]{:S(2)}, u32[]{:S(2)}) collective-permute-start(f32[1088,128]{1,0:T(8,128)S(1)} %get-tuple-element.42), channel_id=1, source_target_pairs={{0,2},{1,3},{2,0},{3,1},{4,6},{5,7},{6,4},{7,5}} | collective-permute-start | bytes 1671176 | tf_op jit(solution)/shard_map/ppermute | solution.py:261
  63.7 11.4 %collective-permute-done.4 = f32[1088,128]{1,0:T(8,128)S(1)} collective-permute-done((f32[1088,128]{1,0:T(8,128)S(1)}, f32[1088,128]{1,0:T(8,128)S(1)}, u32[]{:S(2)}, u32[]{:S(2)}) %collective-permute-start.4) | collective-permute-done | bytes 557088 | tf_op jit(solution)/shard_map/ppermute | solution.py:261
  75.0 0.1 add.23
  75.1 0.0 collective-permute-start.5
  75.1 0.7 collective-permute-done.6
  75.9 11.1 %collective-permute-done.8 = f32[1088,128]{1,0:T(8,128)S(1)} collective-permute-done((f32[1088,128]{1,0:T(8,128)S(1)}, f32[1088,128]{1,0:T(8,128)S(1)}, u32[]{:S(2)}, u32[]{:S(2)}) %collective-permute-start.8) | collective-permute-done | bytes 557088 | tf_op jit(solution)/shard_map/ppermute | solution.py:261
  87.0 0.9 add_add_fusion
  87.9 10.4 %collective-permute-done.3 = f32[1088,128]{1,0:T(8,128)S(1)} collective-permute-done((f32[1088,128]{1,0:T(8,128)S(1)}, f32[1088,128]{1,0:T(8,128)S(1)}, u32[]{:S(2)}, u32[]{:S(2)}) %collective-permute-start.3) | collective-permute-done | bytes 557088 | tf_op jit(solution)/shard_map/ppermute | solution.py:261
  98.3 0.0 collective-permute-done.5
  98.3 0.9 add_multiply_fusion
  99.2 0.0 collective-permute-done.2
  99.2 1.2 %multiply_convert_fusion = bf16[4096,128]{1,0:T(8,128)(2,1)} fusion(f32[4096,128]{1,0:T(8,128)S(1)} %get-tuple-element.39, f32[4096,128]{1,0:T(8,128)S(1)} %collective-permute-done.2), kind=kLoop, calls=%fused_computation | loop fusion | flops 1572864 | bytes 5242880 | tf_op jit(solution)/shard_map/convert_element_type | solution.py:327
Async XLA Ops:
  18.2 16.7 %collective-permute-start = (bf16[1088,128]{1,0:T(8,128)(2,1)S(1)}, bf16[1088,128]{1,0:T(8,128)(2,1)S(1)}, u32[]{:S(2)}, u32[]{:S(2)}) collective-permute-start(bf16[1088,128]{1,0:T(8,128)(2,1)S(1)} %get-tuple-element.32.refs_6_), channel_id=1, source_target_pairs={{0,4},{1,5},{2,6},{3,7},{4,0},{5,1},{6,2},{7,3}} | collective-permute-start | bytes 835592 | tf_op jit(solution)/shard_map/ppermute | solution.py:261
  19.2 15.7 %collective-permute-start.1 = (bf16[1088,128]{1,0:T(8,128)(2,1)S(1)}, bf16[1088,128]{1,0:T(8,128)(2,1)S(1)}, u32[]{:S(2)}, u32[]{:S(2)}) collective-permute-start(bf16[1088,128]{1,0:T(8,128)(2,1)S(1)} %get-tuple-element.33.refs_9_), channel_id=1, source_target_pairs={{0,2},{1,3},{2,0},{3,1},{4,6},{5,7},{6,4},{7,5}} | collective-permute-start | bytes 835592 | tf_op jit(solution)/shard_map/ppermute | solution.py:261
  35.0 4.1 %copy-start = (bf16[1088,1,128]{2,0,1:T(8,128)(2,1)S(1)}, bf16[1088,1,128]{2,0,1:T(8,128)(2,1)}, u32[]{:S(2)}) copy-start(bf16[1088,1,128]{2,0,1:T(8,128)(2,1)} %param.11) | copy-start | bytes 835588
  35.0 4.1 %copy-start.1 = (bf16[1088,1,128]{2,0,1:T(8,128)(2,1)S(1)}, bf16[1088,1,128]{2,0,1:T(8,128)(2,1)}, u32[]{:S(2)}) copy-start(bf16[1088,1,128]{2,0,1:T(8,128)(2,1)} %param.12) | copy-start | bytes 835588
  39.0 22.5 %collective-permute-start.7 = (f32[1088,128]{1,0:T(8,128)S(1)}, f32[1088,128]{1,0:T(8,128)S(1)}, u32[]{:S(2)}, u32[]{:S(2)}) collective-permute-start(f32[1088,128]{1,0:T(8,128)S(1)} %get-tuple-element.48), channel_id=1, source_target_pairs={{0,4},{1,5},{2,6},{3,7},{4,0},{5,1},{6,2},{7,3}} | collective-permute-start | bytes 1671176 | tf_op jit(solution)/shard_map/ppermute | solution.py:261
  49.3 49.9 %collective-permute-start.2 = (f32[4096,128]{1,0:T(8,128)S(1)}, f32[4096,128]{1,0:T(8,128)S(1)}, u32[]{:S(2)}, u32[]{:S(2)}) collective-permute-start(f32[4096,128]{1,0:T(8,128)S(1)} %get-tuple-element.40), channel_id=1, source_target_pairs={{0,1},{1,0},{2,3},{3,2},{4,5},{5,4},{6,7},{7,6}} | collective-permute-start | bytes 6291464 | tf_op jit(solution)/shard_map/ppermute | solution.py:261
  58.0 17.1 %collective-permute-start.4 = (f32[1088,128]{1,0:T(8,128)S(1)}, f32[1088,128]{1,0:T(8,128)S(1)}, u32[]{:S(2)}, u32[]{:S(2)}) collective-permute-start(f32[1088,128]{1,0:T(8,128)S(1)} %get-tuple-element.44), channel_id=1, source_target_pairs={{0,2},{1,3},{2,0},{3,1},{4,6},{5,7},{6,4},{7,5}} | collective-permute-start | bytes 1671176 | tf_op jit(solution)/shard_map/ppermute | solution.py:261
  61.6 14.3 %collective-permute-start.6 = (f32[1088,128]{1,0:T(8,128)S(1)}, f32[1088,128]{1,0:T(8,128)S(1)}, u32[]{:S(2)}, u32[]{:S(2)}) collective-permute-start(f32[1088,128]{1,0:T(8,128)S(1)} %get-tuple-element.46), channel_id=1, source_target_pairs={{0,4},{1,5},{2,6},{3,7},{4,0},{5,1},{6,2},{7,3}} | collective-permute-start | bytes 1671176 | tf_op jit(solution)/shard_map/ppermute | solution.py:261
  61.6 25.3 %collective-permute-start.8 = (f32[1088,128]{1,0:T(8,128)S(1)}, f32[1088,128]{1,0:T(8,128)S(1)}, u32[]{:S(2)}, u32[]{:S(2)}) collective-permute-start(f32[1088,128]{1,0:T(8,128)S(1)} %add.26), channel_id=1, source_target_pairs={{0,2},{1,3},{2,0},{3,1},{4,6},{5,7},{6,4},{7,5}} | collective-permute-start | bytes 1671176 | tf_op jit(solution)/shard_map/ppermute | solution.py:261
  61.7 36.6 %collective-permute-start.3 = (f32[1088,128]{1,0:T(8,128)S(1)}, f32[1088,128]{1,0:T(8,128)S(1)}, u32[]{:S(2)}, u32[]{:S(2)}) collective-permute-start(f32[1088,128]{1,0:T(8,128)S(1)} %get-tuple-element.42), channel_id=1, source_target_pairs={{0,2},{1,3},{2,0},{3,1},{4,6},{5,7},{6,4},{7,5}} | collective-permute-start | bytes 1671176 | tf_op jit(solution)/shard_map/ppermute | solution.py:261
  75.1 23.2 %collective-permute-start.5 = (f32[1088,128]{1,0:T(8,128)S(1)}, f32[1088,128]{1,0:T(8,128)S(1)}, u32[]{:S(2)}, u32[]{:S(2)}) collective-permute-start(f32[1088,128]{1,0:T(8,128)S(1)} %add.23), channel_id=1, source_target_pairs={{0,4},{1,5},{2,6},{3,7},{4,0},{5,1},{6,2},{7,3}} | collective-permute-start | bytes 1671176 | tf_op jit(solution)/shard_map/ppermute | solution.py:261

commit v3 on v2

--- a/solution.py
+++ b/solution.py
@@ -14,7 +14,8 @@
 VMEM, SMEM = pltpu.VMEM, pltpu.SMEM
 HIGHEST = lax.Precision.HIGHEST
 KT = 256
-UNROLL = 4
+SMALL = 128
+MAIN, MAIN_SMALL, TAIL = 6, 6, 2
 
 
 def flip(me, bit):
@@ -116,37 +117,46 @@
         copy.wait_send()
 
 
-def split_kernel(dq_ref, own_ref, other_ref):
-    n_sub, _, rows = dq_ref.shape
-    half = rows // 2
-    core = lax.rem(lax.axis_index('cp'), 2)
-    mine = pl.multiple_of(core * half, half)
-    theirs = pl.multiple_of((1 - core) * half, half)
-
-    def put(t, c):
-        r0 = pl.multiple_of(t * half, half)
-        other_ref[pl.ds(r0, half), :] = dq_ref[t, :, pl.ds(theirs, half)].T
-        own_ref[pl.ds(r0, half), :] = dq_ref[t, :, pl.ds(mine, half)].T
+def finish_kernel(own_ref, got_ref, out_ref, *, scale):
+    half = own_ref.shape[2]
+
+    step = 4
+
+    def put(i, c):
+        for u in range(step):
+            t = i * step + u
+            total = (own_ref[t] + got_ref[t]) * scale
+            out_ref[pl.ds(pl.multiple_of(t * half, half), half), :] = total.T.astype(jnp.bfloat16)
         return c
 
-    lax.fori_loop(0, n_sub, put, 0)
-
-
-def attn_kernel(*refs, blocks, row0, n_keys, outs, has_dq, scale, blk, pre, sub_len, loc, heads):
+    lax.fori_loop(0, own_ref.shape[0] // step, put, 0)
+
+
+def attn_kernel(*refs, blocks, n_keys, outs, has_dq, last, scale, blk, pre, sub_len, loc, heads):
     first_ref, q_ref, do_ref, lse_ref, delta_ref, start_ref = refs[:6]
     nb = len(blocks)
     k_in, v_in, refs = refs[6:6 + nb], refs[6 + nb:6 + 2 * nb], refs[6 + 2 * nb:]
     if has_dq:
         dq_in, refs = refs[0], refs[1:]
-    dq_ref, grad_out, refs = refs[0], refs[1:1 + len(outs)], refs[1 + len(outs):]
-    it_t, it_k, it_lo, it_base, p_ref, ds_ref, kpos_ref, k_ref, v_ref, dk_ref, dv_ref = refs
+    n_dq = 2 if last else 1
+    dq_out, grad_out, refs = refs[:n_dq], refs[n_dq:n_dq + len(outs)], refs[n_dq + len(outs):]
+    it_t, it_k, it_lo, it_base, p_ref, ds_ref, kpos_ref, refs = *refs[:7], refs[7:]
+    if last:
+        dq_ref, refs = refs[0], refs[1:]
+    else:
+        dq_ref = dq_out[0]
+    if nb == 1:
+        k_ref, v_ref, dk_ref, dv_ref = k_in[0], v_in[0], grad_out[0], grad_out[1]
+    else:
+        k_ref, v_ref, dk_ref, dv_ref = refs
     me = lax.axis_index('cp')
     n_sub, half = lse_ref.shape[1], lse_ref.shape[2]
     rows = 2 * half
     pos0 = pre + (me // 2) * 2 * loc
-    for b in range(nb):
-        k_ref[b * n_keys:(b + 1) * n_keys, :] = k_in[b][row0:row0 + n_keys, :]
-        v_ref[b * n_keys:(b + 1) * n_keys, :] = v_in[b][row0:row0 + n_keys, :]
+    if nb > 1:
+        for b in range(nb):
+            k_ref[b * n_keys:(b + 1) * n_keys, :] = k_in[b][...]
+            v_ref[b * n_keys:(b + 1) * n_keys, :] = v_in[b][...]
     dk_ref[...] = jnp.zeros_like(dk_ref)
     dv_ref[...] = jnp.zeros_like(dv_ref)
     if has_dq:
@@ -154,39 +164,46 @@
     else:
         dq_ref[...] = jnp.zeros_like(dq_ref)
 
-    n_items = 0
+    cap = it_t.shape[0] // 2
+
+    def put_item(m, t, b, row, lo, blo, kt):
+        it_t[m] = t
+        it_k[m] = b * n_keys + jnp.minimum(row, n_keys - kt)
+        it_lo[m] = lo
+        it_base[m] = blo - b * n_keys
+
+    n_items, n_small = 0, 0
     for b, bits in enumerate(blocks):
         owner = me
         for bit in bits:
             owner = flip(owner, bit)
-        blo = owner * blk + row0
+        blo = owner * blk
 
         def more(c, blo=blo):
             return (c[0] < n_sub) & (first_ref[0, jnp.minimum(c[0], n_sub - 1)] < blo + n_keys)
 
         def add_tile(c, b=b, blo=blo):
-            t, n = c
+            t, n, ns = c
             lo = jnp.maximum(first_ref[0, t], blo)
             hi = jnp.minimum(pos0 + t * sub_len + 2 * loc - 1, blo + n_keys - 1)
             off = (lo - blo) // 16 * 16
-            cnt = (hi - blo - off) // KT + 1
+            length = hi - blo - off + 1
+            full = length // KT
+            rest = length - full * KT
+            cnt = full + jnp.where(rest > SMALL, 1, 0)
 
             def add_item(i, m):
-                it_t[m] = t
-                it_k[m] = b * n_keys + jnp.minimum(off + i * KT, n_keys - KT)
-                it_lo[m] = blo + off + i * KT
-                it_base[m] = blo - b * n_keys
+                put_item(m, t, b, off + i * KT, blo + off + i * KT, blo, KT)
                 return m + 1
 
-            return t + 1, lax.fori_loop(0, cnt, add_item, n)
+            put_item(cap + ns, t, b, off + full * KT, blo + off + full * KT, blo, SMALL)
+            ns = ns + jnp.where((rest > 0) & (rest <= SMALL), 1, 0)
+            return t + 1, lax.fori_loop(0, cnt, add_item, n), ns
 
         t_first = jnp.maximum(blo - pos0 - 2 * loc + sub_len, 0) // sub_len
-        n_items = lax.while_loop(more, add_tile, (t_first, n_items))[1]
-    for u in range(UNROLL - 1):
-        it_t[n_items + u] = 0
-        it_k[n_items + u] = 0
-        it_lo[n_items + u] = 1 << 30
-        it_base[n_items + u] = 0
+        _, n_items, n_small = lax.while_loop(more, add_tile, (t_first, n_items, n_small))
+    for n in (n_items, cap + n_small):
+        put_item(n, 0, 0, 0, 1 << 30, 0, KT)
 
     def two(ref, t):
         return jnp.concatenate([ref[0, pl.ds(t, 1), :], ref[1, pl.ds(t, 1), :]], axis=1)
@@ -195,21 +212,21 @@
     zero = jnp.zeros((16, rows), jnp.bfloat16)
     kpos_ref[...] = lax.broadcasted_iota(jnp.int32, (KT, rows), 0).astype(jnp.float32).astype(jnp.bfloat16)
 
-    def item(w, u):
-        m = w * UNROLL + u
+    def item(m):
         t = it_t[m]
         k0 = pl.multiple_of(it_k[m], 16)
         r0 = pl.multiple_of(t * half, half)
         q = jnp.concatenate([q_ref[0, pl.ds(r0, half), :], q_ref[1, pl.ds(r0, half), :]], axis=0)
         do = jnp.concatenate([do_ref[0, pl.ds(r0, half), :], do_ref[1, pl.ds(r0, half), :]], axis=0)
-        return m, t, k0, q, do
-
-    def scores(w):
+        return t, k0, q, do
+
+    def scores(first, n, kt):
         out = []
-        for u in range(UNROLL):
-            m, t, k0, q, do = item(w, u)
-            s = lax.dot_general(k_ref[pl.ds(k0, KT), :], q, NT, preferred_element_type=jnp.float32)
-            dp = lax.dot_general(v_ref[pl.ds(k0, KT), :], do, NT, preferred_element_type=jnp.float32)
+        for u in range(n):
+            m = first + u
+            t, k0, q, do = item(m)
+            s = lax.dot_general(k_ref[pl.ds(k0, kt), :], q, NT, preferred_element_type=jnp.float32)
+            dp = lax.dot_general(v_ref[pl.ds(k0, kt), :], do, NT, preferred_element_type=jnp.float32)
             lo = jnp.maximum(two(start_ref, t), it_lo[m]) - (k0 + it_base[m])
             qpos = lane // heads + (pos0 + t * sub_len - k0 - it_base[m])
             lo = packed(jnp.clip(lo, 0, KT))
@@ -220,10 +237,10 @@
     def packed(x):
         return jnp.broadcast_to(x.astype(jnp.float32), (16, rows)).astype(jnp.bfloat16)
 
-    def probs(parts):
-        for u in range(UNROLL):
+    def probs(parts, kt):
+        for u in range(len(parts)):
             s, dp, lo, qpos, lse, delta = parts[u]
-            for g in range(KT // 16):
+            for g in range(kt // 16):
                 r = slice(16 * g, 16 * g + 16)
                 kpos = kpos_ref[r, :]
                 allowed = (kpos >= lo) & (kpos <= qpos)
@@ -232,23 +249,44 @@
                 p_ref[u, r, :] = jnp.where(allowed, p.astype(jnp.bfloat16), zero)
                 ds_ref[u, r, :] = jnp.where(allowed, ds.astype(jnp.bfloat16), zero)
 
-    def grads(w):
-        for u in range(UNROLL):
-            _, t, k0, q, do = item(w, u)
-            p, ds = p_ref[u], ds_ref[u]
-            dv_ref[pl.ds(k0, KT), :] += jnp.dot(p, do, preferred_element_type=jnp.float32)
-            dk_ref[pl.ds(k0, KT), :] += jnp.dot(ds, q, preferred_element_type=jnp.float32)
-            dq_ref[t] += jnp.dot(k_ref[pl.ds(k0, KT), :].T, ds, preferred_element_type=jnp.float32)
-
-    def body(w, c):
-        probs(scores(w))
-        grads(w)
-        return c
-
-    lax.fori_loop(0, (n_items + UNROLL - 1) // UNROLL, body, 0)
-    for ref, (kind, which) in zip(grad_out, outs):
-        acc = dk_ref if kind == 'k' else dv_ref
-        ref[...] = acc[which[0] * n_keys:(which[-1] + 1) * n_keys, :]
+    def grads(first, n, kt):
+        for u in range(n):
+            t, k0, q, do = item(first + u)
+            p, ds = p_ref[u, :kt, :], ds_ref[u, :kt, :]
+            dv_ref[pl.ds(k0, kt), :] += jnp.dot(p, do, preferred_element_type=jnp.float32)
+            dk_ref[pl.ds(k0, kt), :] += jnp.dot(ds, q, preferred_element_type=jnp.float32)
+            dq_ref[t] += jnp.dot(k_ref[pl.ds(k0, kt), :].T, ds, preferred_element_type=jnp.float32)
+
+    def loop(first, n, count, kt):
+        def body(w, c):
+            m = first + w * n
+            probs(scores(m, n, kt), kt)
+            grads(m, n, kt)
+            return c
+
+        lax.fori_loop(0, count, body, 0)
+
+    n_main = n_items // MAIN
+    loop(0, MAIN, n_main, KT)
+    loop(n_main * MAIN, TAIL, (n_items - n_main * MAIN + TAIL - 1) // TAIL, KT)
+    n_main = n_small // MAIN_SMALL
+    loop(cap, MAIN_SMALL, n_main, SMALL)
+    loop(cap + n_main * MAIN_SMALL, TAIL, (n_small - n_main * MAIN_SMALL + TAIL - 1) // TAIL, SMALL)
+    if nb > 1:
+        for ref, (kind, which) in zip(grad_out, outs):
+            acc = dk_ref if kind == 'k' else dv_ref
+            ref[...] = acc[which[0] * n_keys:(which[-1] + 1) * n_keys, :]
+    if last:
+        core = lax.rem(me, 2)
+        mine = pl.multiple_of(core * half, half)
+        theirs = pl.multiple_of((1 - core) * half, half)
+
+        def put(t, c):
+            dq_out[0][t] = dq_ref[t, :, pl.ds(mine, half)]
+            dq_out[1][t] = dq_ref[t, :, pl.ds(theirs, half)]
+            return c
+
+        lax.fori_loop(0, n_sub, put, 0)
 
 
 def solution(mesh):
@@ -277,21 +315,24 @@
         k_own, v_own = key_act.reshape(blk, d), value_act.reshape(blk, d)
         pad = (n_keys // 128 + 7) // 8 * 8
         acc = sds((n_sub, d, 2 * half), f32)
-        dq_out = sds((n_sub * half, d), f32)
+        dq_half = sds((n_sub, d, half), f32)
         cost = pl.CostEstimate(flops=2 * 10 ** 9, bytes_accessed=10 ** 7, transcendentals=10 ** 6)
 
-        def attend(keys, values, dq, blocks, row0, n_rows, outs):
+        def attend(keys, values, dq, blocks, outs, last=False):
             nb = len(blocks)
             ins = [first, q2, do2, lse2, delta, start, *keys, *values] + ([dq] if dq is not None else [])
-            cap = nb * n_sub * (-(-n_rows // KT) + 1) + UNROLL
-            kv = (nb * n_rows, d)
+            cap = nb * n_sub * (-(-blk // KT) + 1) + TAIL
+            kv = (nb * blk, d)
+            dq_shapes = (dq_half, dq_half) if last else (acc,)
+            scratch = [SMEM((2 * cap,), i32)] * 4 + [VMEM((MAIN, KT, 2 * half), bf16)] * 2 + [VMEM((KT, 2 * half), bf16)]
+            scratch += [VMEM((n_sub, d, 2 * half), f32)] if last else []
+            scratch += [VMEM(kv, bf16)] * 2 + [VMEM(kv, f32)] * 2 if nb > 1 else []
             return pl.pallas_call(
-                functools.partial(attn_kernel, blocks=blocks, row0=row0, n_keys=n_rows, outs=outs, has_dq=dq is not None,
+                functools.partial(attn_kernel, blocks=blocks, n_keys=blk, outs=outs, has_dq=dq is not None, last=last,
                                   scale=scale, blk=blk, **dims),
-                out_shape=(acc,) + tuple(sds((len(w) * n_rows, d), f32) for _, w in outs),
-                in_specs=[sm] + [vm] * (len(ins) - 1), out_specs=(vm,) * (1 + len(outs)),
-                scratch_shapes=[SMEM((cap,), i32)] * 4 + [VMEM((UNROLL, KT, 2 * half), bf16)] * 2 + [VMEM((KT, 2 * half), bf16)]
-                + [VMEM(kv, bf16)] * 2 + [VMEM(kv, f32)] * 2,
+                out_shape=dq_shapes + tuple(sds((len(w) * blk, d), f32) for _, w in outs),
+                in_specs=[sm] + [vm] * (len(ins) - 1), out_specs=(vm,) * (len(dq_shapes) + len(outs)),
+                scratch_shapes=scratch,
                 compiler_params=pltpu.CompilerParams(vmem_limit_bytes=28 * 2 ** 20),
                 cost_estimate=cost, name='attn_bwd')(*ins)
 
@@ -311,20 +352,20 @@
         vd = swap(vy, 2)
         both = (('k', (0,)), ('v', (0,)))
         four = (('k', (0,)), ('k', (1,)), ('v', (0,)), ('v', (1,)))
-        dq, dk_x, dk_y, dv_x, dv_y = attend([kx, ky], [vx, vy], None, ((2,), (4,)), 0, blk, four)
+        dq, dk_x, dk_y, dv_x, dv_y = attend([kx, ky], [vx, vy], None, ((2,), (4,)), four)
         got_ko = swap(dk_x, 2)
         got_vo = swap(dv_y, 4)
-        dq, dk_d, dv_d = attend([kd], [vd], dq, ((2, 4),), 0, blk, both)
+        dq, dk_d, dv_d = attend([kd], [vd], dq, ((2, 4),), both)
         got_ky = swap(dk_d, 2)
         got_vx = swap(dv_d, 4)
-        dq, dk_o, dv_o = attend([k_own], [v_own], dq, ((),), 0, blk, both)
+        dq_own, dq_other, dk_o, dv_o = attend([k_own], [v_own], dq, ((),), both, last=True)
         last_k = swap(dk_y + got_ky, 4)
         last_v = swap(dv_x + got_vx, 2)
-        dq_own, dq_other = pl.pallas_call(
-            split_kernel, out_shape=(dq_out, dq_out), in_specs=[vm], out_specs=(vm, vm),
-            compiler_params=pltpu.CompilerParams(vmem_limit_bytes=28 * 2 ** 20), name='split_dq')(dq)
         got_dq = swap(dq_other, 1)
-        d_query = ((dq_own + got_dq) * scale).astype(bf16)
+        d_query = pl.pallas_call(
+            functools.partial(finish_kernel, scale=scale), out_shape=sds((n_sub * half, d), bf16), in_specs=[vm, vm], out_specs=vm,
+            compiler_params=pltpu.CompilerParams(vmem_limit_bytes=28 * 2 ** 20),
+            cost_estimate=cost, name='finish_dq')(dq_own, got_dq)
         d_key = (dk_o + got_ko + last_k) * scale
         d_value = dv_o + got_vo + last_v
         return d_query.reshape(query.shape), d_key.reshape(key_act.shape), d_value.reshape(value_act.shape)

time: 101 us -> 93.5 us (0.926)
  Pallas kernels: 46.5 us -> 43.2 us
  starting transfers between devices: 16.4 us -> 13.9 us
  other arithmetic: 3.14 us -> 1.89 us
    pallas_call x4, Pallas kernels: 28.9 us -> 25.6 us  [the longest x3 23.7 us: attend(): pl.pallas_call(functools.partial(attn_kernel, blocks=blocks, n_keys=blk,...]
    ppermute x9, starting transfers between devices: 16.4 us -> 13.9 us  [swap(): return lax.ppermute(x, 'cp', [(i, i ^ bits) for i in range(cp)])]
    convert_element_type x1 -> x0, other arithmetic: 1.24 us -> none  [local_backward(): d_query = ((dq_own + got_dq) * scale).astype(bf16)]
  transfers between devices with their start and end apart: 9 -> 9, of which waited for: 4 -> 4; matrix products, arithmetic and copies ran while one was open for 2% -> 2% of each run, Pallas kernels for 25% -> 22%
where the time goes in v3:
time: 93.5 us; the launch traced here: 93.3 us
  Pallas kernels  43.2 us (46%)
  waiting for transfers between devices  33.6 us (36%)
  starting transfers between devices  13.9 us (15%)
  other arithmetic  1.89 us (2%)
    ppermute x9, waiting for transfers between devices, swap(): return lax.ppermute(x, 'cp', [(i, i ^ bits) for i in range(cp)])  33.6 us
    pallas_call x3, Pallas kernels, attend(): pl.pallas_call(functools.partial(attn_kernel, blocks=blocks, n_keys=blk,...  23.7 us
    pallas_call x1, Pallas kernels, local_backward(): pl.pallas_call(functools.partial(prep_kernel, **dims), out_shape=tuple([s...  17.6 us
    ppermute x9, starting transfers between devices, swap(): return lax.ppermute(x, 'cp', [(i, i ^ bits) for i in range(cp)])  13.9 us
    pallas_call x1, Pallas kernels, local_backward(): pl.pallas_call(functools.partial(finish_kernel, scale=scale), out_shape=s...  1.89 us
  transfers between devices with their start and end apart: 9, of which 4 were waited for; matrix products, arithmetic and copies ran while one was open for 2% of the time, Pallas kernels for 22%

profile of v3, /device:TPU:0, one launch (start us, length us, event | category | flops | bytes accessed | tf_op | source)
XLA Modules:
  0.0 93.3 jit_solution(7675638190779613350)
XLA Ops:
  0.6 17.6 %prep.1 = (bf16[1088,128]{1,0:T(8,128)(2,1)S(1)}, bf16[1088,128]{1,0:T(8,128)(2,1)S(1)}, bf16[1088,128]{1,0:T(8,128)(2,1)S(1)}, bf16[1088,128]{1,0:T(8,128)(2,1)...) custom-call(bf16[1088,128]{1,0:T(8,128)(2,1)} %bitcast.14, ...), custom_call_target="tpu_custom_call" | custom-call | tf_op jit(solution)/shard_map/prep/pallas_call | solution.py:339
  18.2 1.0 %collective-permute-start = (bf16[1088,128]{1,0:T(8,128)(2,1)S(1)}, bf16[1088,128]{1,0:T(8,128)(2,1)S(1)}, u32[]{:S(2)}, u32[]{:S(2)}) collective-permute-start(bf16[1088,128]{1,0:T(8,128)(2,1)S(1)} %get-tuple-element.31.refs_6_), channel_id=1, source_target_pairs={{0,4},{1,5},{2,6},{3,7},{4,0},{5,1},{6,2},{7,3}} | collective-permute-start | bytes 835592 | tf_op jit(solution)/shard_map/ppermute | solution.py:299
  19.2 1.1 %collective-permute-start.1 = (bf16[1088,128]{1,0:T(8,128)(2,1)S(1)}, bf16[1088,128]{1,0:T(8,128)(2,1)S(1)}, u32[]{:S(2)}, u32[]{:S(2)}) collective-permute-start(bf16[1088,128]{1,0:T(8,128)(2,1)S(1)} %get-tuple-element.32.refs_9_), channel_id=1, source_target_pairs={{0,2},{1,3},{2,0},{3,1},{4,6},{5,7},{6,4},{7,5}} | collective-permute-start | bytes 835592 | tf_op jit(solution)/shard_map/ppermute | solution.py:299
  20.3 12.7 %attn_bwd.3 = (f32[32,128,256]{2,1,0:T(8,128)S(1)}, f32[1088,128]{1,0:T(8,128)S(1)}, f32[1088,128]{1,0:T(8,128)S(1)}, f32[1088,128]{1,0:T(8,128)S(1)}, f32[1088,128]{1,0:T(8,128)S(1)}) custom-call(s32[8,32]{1,0:T(8,128)S(1)} %get-tuple-element.25.refs_0_, bf16[2,4096,128]{2,1,0:T(8,128)(2,1)S(1)} %get-tuple-element.26.refs_1_, ...), custom_call_target="tpu_custom_call" | custom-call | flops 2000000000 | bytes 10000000 | tf_op jit(solution)/shard_map/attn_bwd/pallas_call | solution.py:330
  33.0 0.0 collective-permute-done.refs_6_
  33.0 0.0 collective-permute-done.1.refs_7_
  33.1 0.0 copy-start
  33.1 0.0 copy-start.1
  33.1 3.5 %attn_bwd.4 = (f32[32,128,256]{2,1,0:T(8,128)S(1)}, f32[1088,128]{1,0:T(8,128)S(1)}, f32[1088,128]{1,0:T(8,128)S(1)}) custom-call(s32[8,32]{1,0:T(8,128)S(1)} %get-tuple-element.25.refs_0_, bf16[2,4096,128]{2,1,0:T(8,128)(2,1)S(1)} %get-tuple-element.26.refs_1_, bf16[2,4096,128]{2,1,0:T(8,128)(2,1)S(1)} %get-tuple-element.27.refs_2_, ...), custom_call_target="tpu_custom_call" | custom-call | flops 2000000000 | bytes 10000000 | tf_op jit(solution)/shard_map/attn_bwd/pallas_call | solution.py:330
  36.6 0.0 collective-permute-start.7
  36.6 0.0 copy-done
  36.7 0.0 copy-done.1
  36.7 7.4 %attn_bwd.5 = (f32[32,128,128]{2,1,0:T(8,128)S(1)}, f32[32,128,128]{2,1,0:T(8,128)S(1)}, f32[1088,128]{1,0:T(8,128)S(1)}, f32[1088,128]{1,0:T(8,128)S(1)}) custom-call(s32[8,32]{1,0:T(8,128)S(1)} %get-tuple-element.25.refs_0_, bf16[2,4096,128]{2,1,0:T(8,128)(2,1)S(1)} %get-tuple-element.26.refs_1_, bf16[2,4096,128]{2,1,0:T(8,128)(2,1)S(1)} %get-tuple-element.27.refs_2_, ...), custom_call_target="tpu_custom_call" | custom-call | flops 2000000000 | bytes 10000000 | tf_op jit(solution)/shard_map/attn_bwd/pallas_call | solution.py:330
  44.1 5.8 %collective-permute-start.2 = (f32[32,128,128]{2,1,0:T(8,128)S(1)}, f32[32,128,128]{2,1,0:T(8,128)S(1)}, u32[]{:S(2)}, u32[]{:S(2)}) collective-permute-start(f32[32,128,128]{2,1,0:T(8,128)S(1)} %get-tuple-element.38), channel_id=1, source_target_pairs={{0,1},{1,0},{2,3},{3,2},{4,5},{5,4},{6,7},{7,6}} | collective-permute-start | bytes 6291464 | tf_op jit(solution)/shard_map/ppermute | solution.py:299
  49.9 3.9 %collective-permute-start.4 = (f32[1088,128]{1,0:T(8,128)S(1)}, f32[1088,128]{1,0:T(8,128)S(1)}, u32[]{:S(2)}, u32[]{:S(2)}) collective-permute-start(f32[1088,128]{1,0:T(8,128)S(1)} %get-tuple-element.42), channel_id=1, source_target_pairs={{0,2},{1,3},{2,0},{3,1},{4,6},{5,7},{6,4},{7,5}} | collective-permute-start | bytes 1671176 | tf_op jit(solution)/shard_map/ppermute | solution.py:299
  53.9 0.0 collective-permute-start.6
  53.9 0.0 collective-permute-done.7
  53.9 0.1 add.22
  53.9 0.0 collective-permute-start.8
  54.0 2.0 %collective-permute-start.3 = (f32[1088,128]{1,0:T(8,128)S(1)}, f32[1088,128]{1,0:T(8,128)S(1)}, u32[]{:S(2)}, u32[]{:S(2)}) collective-permute-start(f32[1088,128]{1,0:T(8,128)S(1)} %get-tuple-element.40), channel_id=1, source_target_pairs={{0,2},{1,3},{2,0},{3,1},{4,6},{5,7},{6,4},{7,5}} | collective-permute-start | bytes 1671176 | tf_op jit(solution)/shard_map/ppermute | solution.py:299
  56.0 11.4 %collective-permute-done.4 = f32[1088,128]{1,0:T(8,128)S(1)} collective-permute-done((f32[1088,128]{1,0:T(8,128)S(1)}, f32[1088,128]{1,0:T(8,128)S(1)}, u32[]{:S(2)}, u32[]{:S(2)}) %collective-permute-start.4) | collective-permute-done | bytes 557088 | tf_op jit(solution)/shard_map/ppermute | solution.py:299
  67.3 0.1 add.19
  67.4 0.0 collective-permute-start.5
  67.4 0.7 collective-permute-done.6
  68.1 11.1 %collective-permute-done.8 = f32[1088,128]{1,0:T(8,128)S(1)} collective-permute-done((f32[1088,128]{1,0:T(8,128)S(1)}, f32[1088,128]{1,0:T(8,128)S(1)}, u32[]{:S(2)}, u32[]{:S(2)}) %collective-permute-start.8) | collective-permute-done | bytes 557088 | tf_op jit(solution)/shard_map/ppermute | solution.py:299
  79.3 0.9 add_add_fusion
  80.2 10.4 %collective-permute-done.3 = f32[1088,128]{1,0:T(8,128)S(1)} collective-permute-done((f32[1088,128]{1,0:T(8,128)S(1)}, f32[1088,128]{1,0:T(8,128)S(1)}, u32[]{:S(2)}, u32[]{:S(2)}) %collective-permute-start.3) | collective-permute-done | bytes 557088 | tf_op jit(solution)/shard_map/ppermute | solution.py:299
  90.6 0.0 collective-permute-done.5
  90.6 0.9 add_multiply_fusion
  91.5 0.0 collective-permute-done.2.got_ref
  91.5 1.9 %finish_dq.1 = bf16[4096,128]{1,0:T(8,128)(2,1)} custom-call(f32[32,128,128]{2,1,0:T(8,128)S(1)} %get-tuple-element.37.own_ref, f32[32,128,128]{2,1,0:T(8,128)S(1)} %collective-permute-done.2.got_ref), custom_call_target="tpu_custom_call" | custom-call | flops 2000000000 | bytes 10000000 | tf_op jit(solution)/shard_map/finish_dq/pallas_call | solution.py:365
Async XLA Ops:
  18.2 14.8 %collective-permute-start = (bf16[1088,128]{1,0:T(8,128)(2,1)S(1)}, bf16[1088,128]{1,0:T(8,128)(2,1)S(1)}, u32[]{:S(2)}, u32[]{:S(2)}) collective-permute-start(bf16[1088,128]{1,0:T(8,128)(2,1)S(1)} %get-tuple-element.31.refs_6_), channel_id=1, source_target_pairs={{0,4},{1,5},{2,6},{3,7},{4,0},{5,1},{6,2},{7,3}} | collective-permute-start | bytes 835592 | tf_op jit(solution)/shard_map/ppermute | solution.py:299
  19.2 13.8 %collective-permute-start.1 = (bf16[1088,128]{1,0:T(8,128)(2,1)S(1)}, bf16[1088,128]{1,0:T(8,128)(2,1)S(1)}, u32[]{:S(2)}, u32[]{:S(2)}) collective-permute-start(bf16[1088,128]{1,0:T(8,128)(2,1)S(1)} %get-tuple-element.32.refs_9_), channel_id=1, source_target_pairs={{0,2},{1,3},{2,0},{3,1},{4,6},{5,7},{6,4},{7,5}} | collective-permute-start | bytes 835592 | tf_op jit(solution)/shard_map/ppermute | solution.py:299
  33.1 3.6 %copy-start = (bf16[1088,1,128]{2,0,1:T(8,128)(2,1)S(1)}, bf16[1088,1,128]{2,0,1:T(8,128)(2,1)}, u32[]{:S(2)}) copy-start(bf16[1088,1,128]{2,0,1:T(8,128)(2,1)} %param.11) | copy-start | bytes 835588
  33.1 3.6 %copy-start.1 = (bf16[1088,1,128]{2,0,1:T(8,128)(2,1)S(1)}, bf16[1088,1,128]{2,0,1:T(8,128)(2,1)}, u32[]{:S(2)}) copy-start(bf16[1088,1,128]{2,0,1:T(8,128)(2,1)} %param.12) | copy-start | bytes 835588
  36.6 17.2 %collective-permute-start.7 = (f32[1088,128]{1,0:T(8,128)S(1)}, f32[1088,128]{1,0:T(8,128)S(1)}, u32[]{:S(2)}, u32[]{:S(2)}) collective-permute-start(f32[1088,128]{1,0:T(8,128)S(1)} %get-tuple-element.46), channel_id=1, source_target_pairs={{0,4},{1,5},{2,6},{3,7},{4,0},{5,1},{6,2},{7,3}} | collective-permute-start | bytes 1671176 | tf_op jit(solution)/shard_map/ppermute | solution.py:299
  44.1 47.4 %collective-permute-start.2 = (f32[32,128,128]{2,1,0:T(8,128)S(1)}, f32[32,128,128]{2,1,0:T(8,128)S(1)}, u32[]{:S(2)}, u32[]{:S(2)}) collective-permute-start(f32[32,128,128]{2,1,0:T(8,128)S(1)} %get-tuple-element.38), channel_id=1, source_target_pairs={{0,1},{1,0},{2,3},{3,2},{4,5},{5,4},{6,7},{7,6}} | collective-permute-start | bytes 6291464 | tf_op jit(solution)/shard_map/ppermute | solution.py:299
  49.9 17.4 %collective-permute-start.4 = (f32[1088,128]{1,0:T(8,128)S(1)}, f32[1088,128]{1,0:T(8,128)S(1)}, u32[]{:S(2)}, u32[]{:S(2)}) collective-permute-start(f32[1088,128]{1,0:T(8,128)S(1)} %get-tuple-element.42), channel_id=1, source_target_pairs={{0,2},{1,3},{2,0},{3,1},{4,6},{5,7},{6,4},{7,5}} | collective-permute-start | bytes 1671176 | tf_op jit(solution)/shard_map/ppermute | solution.py:299
  53.9 14.3 %collective-permute-start.6 = (f32[1088,128]{1,0:T(8,128)S(1)}, f32[1088,128]{1,0:T(8,128)S(1)}, u32[]{:S(2)}, u32[]{:S(2)}) collective-permute-start(f32[1088,128]{1,0:T(8,128)S(1)} %get-tuple-element.44), channel_id=1, source_target_pairs={{0,4},{1,5},{2,6},{3,7},{4,0},{5,1},{6,2},{7,3}} | collective-permute-start | bytes 1671176 | tf_op jit(solution)/shard_map/ppermute | solution.py:299
  53.9 25.3 %collective-permute-start.8 = (f32[1088,128]{1,0:T(8,128)S(1)}, f32[1088,128]{1,0:T(8,128)S(1)}, u32[]{:S(2)}, u32[]{:S(2)}) collective-permute-start(f32[1088,128]{1,0:T(8,128)S(1)} %add.22), channel_id=1, source_target_pairs={{0,2},{1,3},{2,0},{3,1},{4,6},{5,7},{6,4},{7,5}} | collective-permute-start | bytes 1671176 | tf_op jit(solution)/shard_map/ppermute | solution.py:299
  54.0 36.6 %collective-permute-start.3 = (f32[1088,128]{1,0:T(8,128)S(1)}, f32[1088,128]{1,0:T(8,128)S(1)}, u32[]{:S(2)}, u32[]{:S(2)}) collective-permute-start(f32[1088,128]{1,0:T(8,128)S(1)} %get-tuple-element.40), channel_id=1, source_target_pairs={{0,2},{1,3},{2,0},{3,1},{4,6},{5,7},{6,4},{7,5}} | collective-permute-start | bytes 1671176 | tf_op jit(solution)/shard_map/ppermute | solution.py:299
  67.4 23.2 %collective-permute-start.5 = (f32[1088,128]{1,0:T(8,128)S(1)}, f32[1088,128]{1,0:T(8,128)S(1)}, u32[]{:S(2)}, u32[]{:S(2)}) collective-permute-start(f32[1088,128]{1,0:T(8,128)S(1)} %add.19), channel_id=1, source_target_pairs={{0,4},{1,5},{2,6},{3,7},{4,0},{5,1},{6,2},{7,3}} | collective-permute-start | bytes 1671176 | tf_op jit(solution)/shard_map/ppermute | solution.py:299

commit v4 on v3

--- a/solution.py
+++ b/solution.py
@@ -132,12 +132,13 @@
     lax.fori_loop(0, own_ref.shape[0] // step, put, 0)
 
 
-def attn_kernel(*refs, blocks, n_keys, outs, has_dq, last, scale, blk, pre, sub_len, loc, heads):
+def attn_kernel(*refs, blocks, row0, n_keys, outs, n_prev, has_dq, last, scale, blk, pre, sub_len, loc, heads):
     first_ref, q_ref, do_ref, lse_ref, delta_ref, start_ref = refs[:6]
     nb = len(blocks)
     k_in, v_in, refs = refs[6:6 + nb], refs[6 + nb:6 + 2 * nb], refs[6 + 2 * nb:]
     if has_dq:
         dq_in, refs = refs[0], refs[1:]
+    prev, refs = refs[:n_prev], refs[n_prev:]
     n_dq = 2 if last else 1
     dq_out, grad_out, refs = refs[:n_dq], refs[n_dq:n_dq + len(outs)], refs[n_dq + len(outs):]
     it_t, it_k, it_lo, it_base, p_ref, ds_ref, kpos_ref, refs = *refs[:7], refs[7:]
@@ -155,8 +156,8 @@
     pos0 = pre + (me // 2) * 2 * loc
     if nb > 1:
         for b in range(nb):
-            k_ref[b * n_keys:(b + 1) * n_keys, :] = k_in[b][...]
-            v_ref[b * n_keys:(b + 1) * n_keys, :] = v_in[b][...]
+            k_ref[b * n_keys:(b + 1) * n_keys, :] = k_in[b][row0:row0 + n_keys, :]
+            v_ref[b * n_keys:(b + 1) * n_keys, :] = v_in[b][row0:row0 + n_keys, :]
     dk_ref[...] = jnp.zeros_like(dk_ref)
     dv_ref[...] = jnp.zeros_like(dv_ref)
     if has_dq:
@@ -177,7 +178,7 @@
         owner = me
         for bit in bits:
             owner = flip(owner, bit)
-        blo = owner * blk
+        blo = owner * blk + row0
 
         def more(c, blo=blo):
             return (c[0] < n_sub) & (first_ref[0, jnp.minimum(c[0], n_sub - 1)] < blo + n_keys)
@@ -273,9 +274,13 @@
     loop(cap, MAIN_SMALL, n_main, SMALL)
     loop(cap + n_main * MAIN_SMALL, TAIL, (n_small - n_main * MAIN_SMALL + TAIL - 1) // TAIL, SMALL)
     if nb > 1:
-        for ref, (kind, which) in zip(grad_out, outs):
+        for ref, (kind, b, i) in zip(grad_out, outs):
             acc = dk_ref if kind == 'k' else dv_ref
-            ref[...] = acc[which[0] * n_keys:(which[-1] + 1) * n_keys, :]
+            if i is None:
+                ref[...] = acc[b * n_keys:(b + 1) * n_keys, :]
+            else:
+                ref[0:row0, :] = prev[i][...]
+                ref[row0:row0 + n_keys, :] = acc[b * n_keys:(b + 1) * n_keys, :]
     if last:
         core = lax.rem(me, 2)
         mine = pl.multiple_of(core * half, half)
@@ -318,19 +323,20 @@
         dq_half = sds((n_sub, d, half), f32)
         cost = pl.CostEstimate(flops=2 * 10 ** 9, bytes_accessed=10 ** 7, transcendentals=10 ** 6)
 
-        def attend(keys, values, dq, blocks, outs, last=False):
+        def attend(keys, values, dq, blocks, outs, row0=0, n_rows=blk, prev=(), last=False):
             nb = len(blocks)
-            ins = [first, q2, do2, lse2, delta, start, *keys, *values] + ([dq] if dq is not None else [])
-            cap = nb * n_sub * (-(-blk // KT) + 1) + TAIL
-            kv = (nb * blk, d)
+            ins = [first, q2, do2, lse2, delta, start, *keys, *values] + ([dq] if dq is not None else []) + list(prev)
+            cap = nb * n_sub * (-(-n_rows // KT) + 1) + TAIL
+            kv = (nb * n_rows, d)
             dq_shapes = (dq_half, dq_half) if last else (acc,)
             scratch = [SMEM((2 * cap,), i32)] * 4 + [VMEM((MAIN, KT, 2 * half), bf16)] * 2 + [VMEM((KT, 2 * half), bf16)]
             scratch += [VMEM((n_sub, d, 2 * half), f32)] if last else []
             scratch += [VMEM(kv, bf16)] * 2 + [VMEM(kv, f32)] * 2 if nb > 1 else []
             return pl.pallas_call(
-                functools.partial(attn_kernel, blocks=blocks, n_keys=blk, outs=outs, has_dq=dq is not None, last=last,
+                functools.partial(attn_kernel, blocks=blocks, row0=row0, n_keys=n_rows, outs=outs, n_prev=len(prev),
+                                  has_dq=dq is not None, last=last,
                                   scale=scale, blk=blk, **dims),
-                out_shape=dq_shapes + tuple(sds((len(w) * blk, d), f32) for _, w in outs),
+                out_shape=dq_shapes + tuple(sds((n_rows if i is None else row0 + n_rows, d), f32) for _, _, i in outs),
                 in_specs=[sm] + [vm] * (len(ins) - 1), out_specs=(vm,) * (len(dq_shapes) + len(outs)),
                 scratch_shapes=scratch,
                 compiler_params=pltpu.CompilerParams(vmem_limit_bytes=28 * 2 ** 20),
@@ -350,24 +356,30 @@
             row_lse.transpose(0, 2, 1), doc_ids.reshape(n_keys // 128, 128))])
         kd = swap(kx, 4)
         vd = swap(vy, 2)
-        both = (('k', (0,)), ('v', (0,)))
-        four = (('k', (0,)), ('k', (1,)), ('v', (0,)), ('v', (1,)))
-        dq, dk_x, dk_y, dv_x, dv_y = attend([kx, ky], [vx, vy], None, ((2,), (4,)), four)
-        got_ko = swap(dk_x, 2)
-        got_vo = swap(dv_y, 4)
+        both = (('k', 0, None), ('v', 0, None))
+        sides = ((2,), (4,))
+        cut = blk // KT // 2 * KT
+        four = (('k', 0, None), ('v', 1, None), ('k', 1, None), ('v', 0, None))
+        dq, dk_xa, dv_ya, dk_ya, dv_xa = attend([kx, ky], [vx, vy], None, sides, four, 0, cut)
+        got_ka = swap(dk_xa, 2)
+        got_va = swap(dv_ya, 4)
         dq, dk_d, dv_d = attend([kd], [vd], dq, ((2, 4),), both)
         got_ky = swap(dk_d, 2)
         got_vx = swap(dv_d, 4)
-        dq_own, dq_other, dk_o, dv_o = attend([k_own], [v_own], dq, ((),), both, last=True)
+        four = (('k', 0, None), ('v', 1, None), ('k', 1, 0), ('v', 0, 1))
+        dq, dk_xb, dv_yb, dk_y, dv_x = attend([kx, ky], [vx, vy], dq, sides, four, cut, blk - cut, (dk_ya, dv_xa))
+        got_kb = swap(dk_xb, 2)
+        got_vb = swap(dv_yb, 4)
         last_k = swap(dk_y + got_ky, 4)
         last_v = swap(dv_x + got_vx, 2)
+        dq_own, dq_other, dk_o, dv_o = attend([k_own], [v_own], dq, ((),), both, last=True)
         got_dq = swap(dq_other, 1)
         d_query = pl.pallas_call(
             functools.partial(finish_kernel, scale=scale), out_shape=sds((n_sub * half, d), bf16), in_specs=[vm, vm], out_specs=vm,
             compiler_params=pltpu.CompilerParams(vmem_limit_bytes=28 * 2 ** 20),
             cost_estimate=cost, name='finish_dq')(dq_own, got_dq)
-        d_key = (dk_o + got_ko + last_k) * scale
-        d_value = dv_o + got_vo + last_v
+        d_key = (dk_o + jnp.concatenate([got_ka, got_kb]) + last_k) * scale
+        d_value = dv_o + jnp.concatenate([got_va, got_vb]) + last_v
         return d_query.reshape(query.shape), d_key.reshape(key_act.shape), d_value.reshape(value_act.shape)
 
     return jax.shard_map(local_backward, mesh=mesh, in_specs=(q_spec, q_spec, q_spec, lse_spec, kv_spec, kv_spec, P()), out_specs=(q_spec, kv_spec, kv_spec), check_vma=False)

time: 93.5 us -> 92.4 us (0.988)
  waiting for transfers between devices: 33.6 us -> 31.9 us
  Pallas kernels: 43.2 us -> 44.6 us
    ppermute x9 -> x11, waiting for transfers between devices: 33.6 us -> 31.9 us  [swap(): return lax.ppermute(x, 'cp', [(i, i ^ bits) for i in range(cp)])]
    pallas_call x3 -> x4, Pallas kernels: 23.7 us -> 25.1 us  [attend(): pl.pallas_call(functools.partial(attn_kernel, blocks=blocks, row0=row0, n...]
    ppermute x9 -> x11, starting transfers between devices: 13.9 us -> 13.1 us  [swap(): return lax.ppermute(x, 'cp', [(i, i ^ bits) for i in range(cp)])]
  transfers between devices with their start and end apart: 9 -> 11, of which waited for: 4 -> 5; matrix products, arithmetic and copies ran while one was open for 2% -> 2% of each run, Pallas kernels for 22% -> 23%
where the time goes in v4:
time: 92.4 us; the launch traced here: 92.3 us
  Pallas kernels  44.6 us (48%)
  waiting for transfers between devices  31.9 us (35%)
  starting transfers between devices  13.1 us (14%)
  other arithmetic  1.97 us (2%)
    ppermute x11, waiting for transfers between devices, swap(): return lax.ppermute(x, 'cp', [(i, i ^ bits) for i in range(cp)])  31.9 us
    pallas_call x4, Pallas kernels, attend(): pl.pallas_call(functools.partial(attn_kernel, blocks=blocks, row0=row0, n...  25.1 us
    pallas_call x1, Pallas kernels, local_backward(): pl.pallas_call(functools.partial(prep_kernel, **dims), out_shape=tuple([s...  17.6 us
    ppermute x11, starting transfers between devices, swap(): return lax.ppermute(x, 'cp', [(i, i ^ bits) for i in range(cp)])  13.1 us
    pallas_call x1, Pallas kernels, local_backward(): pl.pallas_call(functools.partial(finish_kernel, scale=scale), out_shape=s...  1.89 us
  transfers between devices with their start and end apart: 11, of which 5 were waited for; matrix products, arithmetic and copies ran while one was open for 2% of the time, Pallas kernels for 23%

profile of v4, /device:TPU:0, one launch (start us, length us, event | category | flops | bytes accessed | tf_op | source)
XLA Modules:
  0.0 92.3 jit_solution(14642185197966139857)
XLA Ops:
  0.6 17.6 %prep.1 = (bf16[1088,128]{1,0:T(8,128)(2,1)S(1)}, bf16[1088,128]{1,0:T(8,128)(2,1)S(1)}, bf16[1088,128]{1,0:T(8,128)(2,1)S(1)}, bf16[1088,128]{1,0:T(8,128)(2,1)...) custom-call(bf16[1088,128]{1,0:T(8,128)(2,1)} %bitcast.14, ...), custom_call_target="tpu_custom_call" | custom-call | tf_op jit(solution)/shard_map/prep/pallas_call | solution.py:345
  18.2 1.0 %collective-permute-start = (bf16[1088,128]{1,0:T(8,128)(2,1)S(1)}, bf16[1088,128]{1,0:T(8,128)(2,1)S(1)}, u32[]{:S(2)}, u32[]{:S(2)}) collective-permute-start(bf16[1088,128]{1,0:T(8,128)(2,1)S(1)} %get-tuple-element.36.refs_6_), channel_id=1, source_target_pairs={{0,4},{1,5},{2,6},{3,7},{4,0},{5,1},{6,2},{7,3}} | collective-permute-start | bytes 835592 | tf_op jit(solution)/shard_map/ppermute | solution.py:304
  19.2 1.1 %collective-permute-start.1 = (bf16[1088,128]{1,0:T(8,128)(2,1)S(1)}, bf16[1088,128]{1,0:T(8,128)(2,1)S(1)}, u32[]{:S(2)}, u32[]{:S(2)}) collective-permute-start(bf16[1088,128]{1,0:T(8,128)(2,1)S(1)} %get-tuple-element.39.refs_9_), channel_id=1, source_target_pairs={{0,2},{1,3},{2,0},{3,1},{4,6},{5,7},{6,4},{7,5}} | collective-permute-start | bytes 835592 | tf_op jit(solution)/shard_map/ppermute | solution.py:304
  20.3 7.4 %attn_bwd.4 = (f32[32,128,256]{2,1,0:T(8,128)S(1)}, f32[512,128]{1,0:T(8,128)S(1)}, f32[512,128]{1,0:T(8,128)S(1)}, f32[512,128]{1,0:T(8,128)S(1)}, f32[512,128]{1,0:T(8,128)S(1)}) custom-call(s32[8,32]{1,0:T(8,128)S(1)} %get-tuple-element.30.refs_0_, bf16[2,4096,128]{2,1,0:T(8,128)(2,1)S(1)} %get-tuple-element.31.refs_1_, ...), custom_call_target="tpu_custom_call" | custom-call | flops 2000000000 | bytes 10000000 | tf_op jit(solution)/shard_map/attn_bwd/pallas_call | solution.py:335
  27.7 0.0 collective-permute-done.refs_6_
  27.7 0.0 collective-permute-done.1.refs_7_
  27.7 3.6 %attn_bwd.5 = (f32[32,128,256]{2,1,0:T(8,128)S(1)}, f32[1088,128]{1,0:T(8,128)S(1)}, f32[1088,128]{1,0:T(8,128)S(1)}) custom-call(s32[8,32]{1,0:T(8,128)S(1)} %get-tuple-element.30.refs_0_, bf16[2,4096,128]{2,1,0:T(8,128)(2,1)S(1)} %get-tuple-element.31.refs_1_, bf16[2,4096,128]{2,1,0:T(8,128)(2,1)S(1)} %get-tuple-element.32.refs_2_, ...), custom_call_target="tpu_custom_call" | custom-call | flops 2000000000 | bytes 10000000 | tf_op jit(solution)/shard_map/attn_bwd/pallas_call | solution.py:335
  31.3 4.5 %collective-permute-start.5 = (f32[1088,128]{1,0:T(8,128)S(1)}, f32[1088,128]{1,0:T(8,128)S(1)}, u32[]{:S(2)}, u32[]{:S(2)}) collective-permute-start(f32[1088,128]{1,0:T(8,128)S(1)} %get-tuple-element.51), channel_id=1, source_target_pairs={{0,2},{1,3},{2,0},{3,1},{4,6},{5,7},{6,4},{7,5}} | collective-permute-start | bytes 1671176 | tf_op jit(solution)/shard_map/ppermute | solution.py:304
  35.8 6.7 %attn_bwd.6 = (f32[32,128,256]{2,1,0:T(8,128)S(1)}, f32[576,128]{1,0:T(8,128)S(1)}, f32[576,128]{1,0:T(8,128)S(1)}, f32[1088,128]{1,0:T(8,128)S(1)}, f32[1088,128]{1,0:T(8,128)S(1)}) custom-call(s32[8,32]{1,0:T(8,128)S(1)} %get-tuple-element.30.refs_0_, bf16[2,4096,128]{2,1,0:T(8,128)(2,1)S(1)} %get-tuple-element.31.refs_1_, ...), custom_call_target="tpu_custom_call" | custom-call | flops 2000000000 | bytes 10000000 | tf_op jit(solution)/shard_map/attn_bwd/pallas_call | solution.py:335
  42.6 7.4 %attn_bwd.7 = (f32[32,128,128]{2,1,0:T(8,128)S(1)}, f32[32,128,128]{2,1,0:T(8,128)S(1)}, f32[1088,128]{1,0:T(8,128)S(1)}, f32[1088,128]{1,0:T(8,128)S(1)}) custom-call(s32[8,32]{1,0:T(8,128)S(1)} %get-tuple-element.30.refs_0_, bf16[2,4096,128]{2,1,0:T(8,128)(2,1)S(1)} %get-tuple-element.31.refs_1_, bf16[2,4096,128]{2,1,0:T(8,128)(2,1)S(1)} %get-tuple-element.32.refs_2_, ...), custom_call_target="tpu_custom_call" | custom-call | flops 2000000000 | bytes 10000000 | tf_op jit(solution)/shard_map/attn_bwd/pallas_call | solution.py:335
  50.0 0.0 collective-permute-start.2
  50.0 2.3 %collective-permute-start.9 = (f32[1088,128]{1,0:T(8,128)S(1)}, f32[1088,128]{1,0:T(8,128)S(1)}, u32[]{:S(2)}, u32[]{:S(2)}) collective-permute-start(f32[1088,128]{1,0:T(8,128)S(1)} %get-tuple-element.56), channel_id=1, source_target_pairs={{0,4},{1,5},{2,6},{3,7},{4,0},{5,1},{6,2},{7,3}} | collective-permute-start | bytes 1671176 | tf_op jit(solution)/shard_map/ppermute | solution.py:304
  52.4 0.0 collective-permute-done.5
  52.4 0.1 add.19
  52.4 0.0 collective-permute-start.6
  52.5 0.0 collective-permute-start.4
  52.5 2.0 %collective-permute-start.3 = (f32[512,128]{1,0:T(8,128)S(1)}, f32[512,128]{1,0:T(8,128)S(1)}, u32[]{:S(2)}, u32[]{:S(2)}) collective-permute-start(f32[512,128]{1,0:T(8,128)S(1)} %get-tuple-element.48), channel_id=1, source_target_pairs={{0,2},{1,3},{2,0},{3,1},{4,6},{5,7},{6,4},{7,5}} | collective-permute-start | bytes 786440 | tf_op jit(solution)/shard_map/ppermute | solution.py:304
  54.5 11.3 %collective-permute-done.9 = f32[1088,128]{1,0:T(8,128)S(1)} collective-permute-done((f32[1088,128]{1,0:T(8,128)S(1)}, f32[1088,128]{1,0:T(8,128)S(1)}, u32[]{:S(2)}, u32[]{:S(2)}) %collective-permute-start.9) | collective-permute-done | bytes 557088 | tf_op jit(solution)/shard_map/ppermute | solution.py:304
  65.8 0.1 add.22
  65.9 0.0 collective-permute-start.10
  65.9 1.3 %collective-permute-done.3 = f32[512,128]{1,0:T(8,128)S(1)} collective-permute-done((f32[512,128]{1,0:T(8,128)S(1)}, f32[512,128]{1,0:T(8,128)S(1)}, u32[]{:S(2)}, u32[]{:S(2)}) %collective-permute-start.3) | collective-permute-done | bytes 262176 | tf_op jit(solution)/shard_map/ppermute | solution.py:304
  67.2 1.7 %collective-permute-start.7 = (f32[512,128]{1,0:T(8,128)S(1)}, f32[512,128]{1,0:T(8,128)S(1)}, u32[]{:S(2)}, u32[]{:S(2)}) collective-permute-start(f32[512,128]{1,0:T(8,128)S(1)} %get-tuple-element.53), channel_id=1, source_target_pairs={{0,4},{1,5},{2,6},{3,7},{4,0},{5,1},{6,2},{7,3}} | collective-permute-start | bytes 786440 | tf_op jit(solution)/shard_map/ppermute | solution.py:304
  68.9 0.0 collective-permute-done.4
  68.9 0.3 collective-permute-start.8
  69.2 8.5 %collective-permute-done.6 = f32[1088,128]{1,0:T(8,128)S(1)} collective-permute-done((f32[1088,128]{1,0:T(8,128)S(1)}, f32[1088,128]{1,0:T(8,128)S(1)}, u32[]{:S(2)}, u32[]{:S(2)}) %collective-permute-start.6) | collective-permute-done | bytes 557088 | tf_op jit(solution)/shard_map/ppermute | solution.py:304
  77.8 0.9 fusion.1
  78.7 4.7 %collective-permute-done.7 = f32[512,128]{1,0:T(8,128)S(1)} collective-permute-done((f32[512,128]{1,0:T(8,128)S(1)}, f32[512,128]{1,0:T(8,128)S(1)}, u32[]{:S(2)}, u32[]{:S(2)}) %collective-permute-start.7) | collective-permute-done | bytes 262176 | tf_op jit(solution)/shard_map/ppermute | solution.py:304
  83.4 6.1 %collective-permute-done.8 = f32[576,128]{1,0:T(8,128)S(1)} collective-permute-done((f32[576,128]{1,0:T(8,128)S(1)}, f32[576,128]{1,0:T(8,128)S(1)}, u32[]{:S(2)}, u32[]{:S(2)}) %collective-permute-start.8) | collective-permute-done | bytes 294944 | tf_op jit(solution)/shard_map/ppermute | solution.py:304
  89.5 0.0 collective-permute-done.10
  89.5 0.9 fusion.2
  90.4 0.0 collective-permute-done.2.got_ref
  90.4 1.9 %finish_dq.1 = bf16[4096,128]{1,0:T(8,128)(2,1)} custom-call(f32[32,128,128]{2,1,0:T(8,128)S(1)} %get-tuple-element.45.own_ref, f32[32,128,128]{2,1,0:T(8,128)S(1)} %collective-permute-done.2.got_ref), custom_call_target="tpu_custom_call" | custom-call | flops 2000000000 | bytes 10000000 | tf_op jit(solution)/shard_map/finish_dq/pallas_call | solution.py:377
  (4 shorter events, 0.0 us)
Async XLA Ops:
  18.2 9.4 %collective-permute-start = (bf16[1088,128]{1,0:T(8,128)(2,1)S(1)}, bf16[1088,128]{1,0:T(8,128)(2,1)S(1)}, u32[]{:S(2)}, u32[]{:S(2)}) collective-permute-start(bf16[1088,128]{1,0:T(8,128)(2,1)S(1)} %get-tuple-element.36.refs_6_), channel_id=1, source_target_pairs={{0,4},{1,5},{2,6},{3,7},{4,0},{5,1},{6,2},{7,3}} | collective-permute-start | bytes 835592 | tf_op jit(solution)/shard_map/ppermute | solution.py:304
  19.2 8.5 %collective-permute-start.1 = (bf16[1088,128]{1,0:T(8,128)(2,1)S(1)}, bf16[1088,128]{1,0:T(8,128)(2,1)S(1)}, u32[]{:S(2)}, u32[]{:S(2)}) collective-permute-start(bf16[1088,128]{1,0:T(8,128)(2,1)S(1)} %get-tuple-element.39.refs_9_), channel_id=1, source_target_pairs={{0,2},{1,3},{2,0},{3,1},{4,6},{5,7},{6,4},{7,5}} | collective-permute-start | bytes 835592 | tf_op jit(solution)/shard_map/ppermute | solution.py:304
  31.3 21.1 %collective-permute-start.5 = (f32[1088,128]{1,0:T(8,128)S(1)}, f32[1088,128]{1,0:T(8,128)S(1)}, u32[]{:S(2)}, u32[]{:S(2)}) collective-permute-start(f32[1088,128]{1,0:T(8,128)S(1)} %get-tuple-element.51), channel_id=1, source_target_pairs={{0,2},{1,3},{2,0},{3,1},{4,6},{5,7},{6,4},{7,5}} | collective-permute-start | bytes 1671176 | tf_op jit(solution)/shard_map/ppermute | solution.py:304
  35.8 6.7 %copy-start = (bf16[1088,1,128]{2,0,1:T(8,128)(2,1)S(1)}, bf16[1088,1,128]{2,0,1:T(8,128)(2,1)}, u32[]{:S(2)}) copy-start(bf16[1088,1,128]{2,0,1:T(8,128)(2,1)} %param.11) | copy-start | bytes 835588
  35.8 6.8 %copy-start.1 = (bf16[1088,1,128]{2,0,1:T(8,128)(2,1)S(1)}, bf16[1088,1,128]{2,0,1:T(8,128)(2,1)}, u32[]{:S(2)}) copy-start(bf16[1088,1,128]{2,0,1:T(8,128)(2,1)} %param.12) | copy-start | bytes 835588
  50.0 40.4 %collective-permute-start.2 = (f32[32,128,128]{2,1,0:T(8,128)S(1)}, f32[32,128,128]{2,1,0:T(8,128)S(1)}, u32[]{:S(2)}, u32[]{:S(2)}) collective-permute-start(f32[32,128,128]{2,1,0:T(8,128)S(1)} %get-tuple-element.46), channel_id=1, source_target_pairs={{0,1},{1,0},{2,3},{3,2},{4,5},{5,4},{6,7},{7,6}} | collective-permute-start | bytes 6291464 | tf_op jit(solution)/shard_map/ppermute | solution.py:304
  50.0 15.8 %collective-permute-start.9 = (f32[1088,128]{1,0:T(8,128)S(1)}, f32[1088,128]{1,0:T(8,128)S(1)}, u32[]{:S(2)}, u32[]{:S(2)}) collective-permute-start(f32[1088,128]{1,0:T(8,128)S(1)} %get-tuple-element.56), channel_id=1, source_target_pairs={{0,4},{1,5},{2,6},{3,7},{4,0},{5,1},{6,2},{7,3}} | collective-permute-start | bytes 1671176 | tf_op jit(solution)/shard_map/ppermute | solution.py:304
  52.4 25.4 %collective-permute-start.6 = (f32[1088,128]{1,0:T(8,128)S(1)}, f32[1088,128]{1,0:T(8,128)S(1)}, u32[]{:S(2)}, u32[]{:S(2)}) collective-permute-start(f32[1088,128]{1,0:T(8,128)S(1)} %add.19), channel_id=1, source_target_pairs={{0,4},{1,5},{2,6},{3,7},{4,0},{5,1},{6,2},{7,3}} | collective-permute-start | bytes 1671176 | tf_op jit(solution)/shard_map/ppermute | solution.py:304
  52.5 16.5 %collective-permute-start.4 = (f32[576,128]{1,0:T(8,128)S(1)}, f32[576,128]{1,0:T(8,128)S(1)}, u32[]{:S(2)}, u32[]{:S(2)}) collective-permute-start(f32[576,128]{1,0:T(8,128)S(1)} %get-tuple-element.49), channel_id=1, source_target_pairs={{0,2},{1,3},{2,0},{3,1},{4,6},{5,7},{6,4},{7,5}} | collective-permute-start | bytes 884744 | tf_op jit(solution)/shard_map/ppermute | solution.py:304
  52.5 14.7 %collective-permute-start.3 = (f32[512,128]{1,0:T(8,128)S(1)}, f32[512,128]{1,0:T(8,128)S(1)}, u32[]{:S(2)}, u32[]{:S(2)}) collective-permute-start(f32[512,128]{1,0:T(8,128)S(1)} %get-tuple-element.48), channel_id=1, source_target_pairs={{0,2},{1,3},{2,0},{3,1},{4,6},{5,7},{6,4},{7,5}} | collective-permute-start | bytes 786440 | tf_op jit(solution)/shard_map/ppermute | solution.py:304
  65.9 23.6 %collective-permute-start.10 = (f32[1088,128]{1,0:T(8,128)S(1)}, f32[1088,128]{1,0:T(8,128)S(1)}, u32[]{:S(2)}, u32[]{:S(2)}) collective-permute-start(f32[1088,128]{1,0:T(8,128)S(1)} %add.22), channel_id=1, source_target_pairs={{0,2},{1,3},{2,0},{3,1},{4,6},{5,7},{6,4},{7,5}} | collective-permute-start | bytes 1671176 | tf_op jit(solution)/shard_map/ppermute | solution.py:304
  67.2 16.2 %collective-permute-start.7 = (f32[512,128]{1,0:T(8,128)S(1)}, f32[512,128]{1,0:T(8,128)S(1)}, u32[]{:S(2)}, u32[]{:S(2)}) collective-permute-start(f32[512,128]{1,0:T(8,128)S(1)} %get-tuple-element.53), channel_id=1, source_target_pairs={{0,4},{1,5},{2,6},{3,7},{4,0},{5,1},{6,2},{7,3}} | collective-permute-start | bytes 786440 | tf_op jit(solution)/shard_map/ppermute | solution.py:304
  68.9 20.6 %collective-permute-start.8 = (f32[576,128]{1,0:T(8,128)S(1)}, f32[576,128]{1,0:T(8,128)S(1)}, u32[]{:S(2)}, u32[]{:S(2)}) collective-permute-start(f32[576,128]{1,0:T(8,128)S(1)} %get-tuple-element.54), channel_id=1, source_target_pairs={{0,4},{1,5},{2,6},{3,7},{4,0},{5,1},{6,2},{7,3}} | collective-permute-start | bytes 884744 | tf_op jit(solution)/shard_map/ppermute | solution.py:304

commit v5 on v4

--- a/solution.py
+++ b/solution.py
@@ -130,6 +130,18 @@
         return c
 
     lax.fori_loop(0, own_ref.shape[0] // step, put, 0)
+
+
+def sum_kernel(dk_ref, ka_ref, kb_ref, lk_ref, dv_ref, va_ref, vb_ref, lv_ref, dk_out, dv_out, sum_ref, sem, *, scale, cut):
+    n = dk_ref.shape[0]
+    copies = []
+    for i, (own, a, b, end, out, mul) in enumerate([(dk_ref, ka_ref, kb_ref, lk_ref, dk_out, scale), (dv_ref, va_ref, vb_ref, lv_ref, dv_out, 1.0)]):
+        sum_ref[i, 0:cut, :] = (own[0:cut, :] + a[...] + end[0:cut, :]) * mul
+        sum_ref[i, cut:n, :] = (own[cut:n, :] + b[...] + end[cut:n, :]) * mul
+        copies.append(pltpu.make_async_copy(sum_ref.at[i], out, sem.at[i]))
+        copies[-1].start()
+    for copy in copies:
+        copy.wait()
 
 
 def attn_kernel(*refs, blocks, row0, n_keys, outs, n_prev, has_dq, last, scale, blk, pre, sub_len, loc, heads):
@@ -160,9 +172,9 @@
             v_ref[b * n_keys:(b + 1) * n_keys, :] = v_in[b][row0:row0 + n_keys, :]
     dk_ref[...] = jnp.zeros_like(dk_ref)
     dv_ref[...] = jnp.zeros_like(dv_ref)
-    if has_dq:
+    if last:
         dq_ref[...] = dq_in[...]
-    else:
+    elif not has_dq:
         dq_ref[...] = jnp.zeros_like(dq_ref)
 
     cap = it_t.shape[0] // 2
@@ -320,6 +332,7 @@
         k_own, v_own = key_act.reshape(blk, d), value_act.reshape(blk, d)
         pad = (n_keys // 128 + 7) // 8 * 8
         acc = sds((n_sub, d, 2 * half), f32)
+        kv_out = sds((blk, d), f32)
         dq_half = sds((n_sub, d, half), f32)
         cost = pl.CostEstimate(flops=2 * 10 ** 9, bytes_accessed=10 ** 7, transcendentals=10 ** 6)
 
@@ -338,7 +351,7 @@
                                   scale=scale, blk=blk, **dims),
                 out_shape=dq_shapes + tuple(sds((n_rows if i is None else row0 + n_rows, d), f32) for _, _, i in outs),
                 in_specs=[sm] + [vm] * (len(ins) - 1), out_specs=(vm,) * (len(dq_shapes) + len(outs)),
-                scratch_shapes=scratch,
+                scratch_shapes=scratch, input_output_aliases={6 + 2 * nb: 0} if dq is not None and not last else {},
                 compiler_params=pltpu.CompilerParams(vmem_limit_bytes=28 * 2 ** 20),
                 cost_estimate=cost, name='attn_bwd')(*ins)
 
@@ -378,8 +391,12 @@
             functools.partial(finish_kernel, scale=scale), out_shape=sds((n_sub * half, d), bf16), in_specs=[vm, vm], out_specs=vm,
             compiler_params=pltpu.CompilerParams(vmem_limit_bytes=28 * 2 ** 20),
             cost_estimate=cost, name='finish_dq')(dq_own, got_dq)
-        d_key = (dk_o + jnp.concatenate([got_ka, got_kb]) + last_k) * scale
-        d_value = dv_o + jnp.concatenate([got_va, got_vb]) + last_v
+        d_key, d_value = pl.pallas_call(
+            functools.partial(sum_kernel, scale=scale, cut=cut), out_shape=(kv_out, kv_out), in_specs=[vm] * 8,
+            out_specs=(pl.BlockSpec(memory_space=pltpu.HBM),) * 2,
+            scratch_shapes=[VMEM((2, blk, d), f32), pltpu.SemaphoreType.DMA((2,))],
+            compiler_params=pltpu.CompilerParams(vmem_limit_bytes=28 * 2 ** 20),
+            cost_estimate=cost, name='sum_kv')(dk_o, got_ka, got_kb, last_k, dv_o, got_va, got_vb, last_v)
         return d_query.reshape(query.shape), d_key.reshape(key_act.shape), d_value.reshape(value_act.shape)
 
     return jax.shard_map(local_backward, mesh=mesh, in_specs=(q_spec, q_spec, q_spec, lse_spec, kv_spec, kv_spec, P()), out_specs=(q_spec, kv_spec, kv_spec), check_vma=False)

time: 92.4 us -> 90.3 us (0.977)
  waiting for transfers between devices: 31.9 us -> 29.9 us
  other arithmetic: 1.97 us -> 0.12 us
  starting transfers between devices: 13.1 us -> 14.2 us
    ppermute x11, waiting for transfers between devices: 31.9 us -> 29.9 us  [swap(): return lax.ppermute(x, 'cp', [(i, i ^ bits) for i in range(cp)])]
    pallas_call x0 -> x1, Pallas kernels: none -> 1.14 us  [local_backward(): pl.pallas_call(functools.partial(sum_kernel, scale=scale, cut=cut), out_s...]
    ppermute x11, starting transfers between devices: 13.1 us -> 14.2 us  [swap(): return lax.ppermute(x, 'cp', [(i, i ^ bits) for i in range(cp)])]
  transfers between devices with their start and end apart: 11 -> 11, of which waited for: 5 -> 5; matrix products, arithmetic and copies ran while one was open for 2% -> 0% of each run, Pallas kernels for 23% -> 9%
where the time goes in v5:
time: 90.3 us; the launch traced here: 90.2 us
  Pallas kernels  45.2 us (50%)
  waiting for transfers between devices  29.9 us (33%)
  starting transfers between devices  14.2 us (16%)
    ppermute x11, waiting for transfers between devices, swap(): return lax.ppermute(x, 'cp', [(i, i ^ bits) for i in range(cp)])  29.9 us
    pallas_call x4, Pallas kernels, attend(): pl.pallas_call(functools.partial(attn_kernel, blocks=blocks, row0=row0, n...  24.5 us
    pallas_call x1, Pallas kernels, local_backward(): pl.pallas_call(functools.partial(prep_kernel, **dims), out_shape=tuple([s...  17.6 us
    ppermute x11, starting transfers between devices, swap(): return lax.ppermute(x, 'cp', [(i, i ^ bits) for i in range(cp)])  14.2 us
    pallas_call x1, Pallas kernels, local_backward(): pl.pallas_call(functools.partial(finish_kernel, scale=scale), out_shape=s...  1.93 us
  transfers between devices with their start and end apart: 11, of which 5 were waited for; matrix products, arithmetic and copies ran while one was open for 0% of the time, Pallas kernels for 9%

profile of v5, /device:TPU:0, one launch (start us, length us, event | category | flops | bytes accessed | tf_op | source)
XLA Modules:
  0.0 90.2 jit_solution(15561612207486638616)
XLA Ops:
  0.6 17.6 %prep.1 = (bf16[1088,128]{1,0:T(8,128)(2,1)S(1)}, bf16[1088,128]{1,0:T(8,128)(2,1)S(1)}, bf16[1088,128]{1,0:T(8,128)(2,1)S(1)}, bf16[1088,128]{1,0:T(8,128)(2,1)...) custom-call(bf16[1088,128]{1,0:T(8,128)(2,1)} %bitcast.14, ...), custom_call_target="tpu_custom_call" | custom-call | tf_op jit(solution)/shard_map/prep/pallas_call | solution.py:358
  18.2 1.0 %collective-permute-start = (bf16[1088,128]{1,0:T(8,128)(2,1)S(1)}, bf16[1088,128]{1,0:T(8,128)(2,1)S(1)}, u32[]{:S(2)}, u32[]{:S(2)}) collective-permute-start(bf16[1088,128]{1,0:T(8,128)(2,1)S(1)} %get-tuple-element.38.refs_6_), channel_id=1, source_target_pairs={{0,4},{1,5},{2,6},{3,7},{4,0},{5,1},{6,2},{7,3}} | collective-permute-start | bytes 835592 | tf_op jit(solution)/shard_map/ppermute | solution.py:316
  19.2 1.1 %collective-permute-start.1 = (bf16[1088,128]{1,0:T(8,128)(2,1)S(1)}, bf16[1088,128]{1,0:T(8,128)(2,1)S(1)}, u32[]{:S(2)}, u32[]{:S(2)}) collective-permute-start(bf16[1088,128]{1,0:T(8,128)(2,1)S(1)} %get-tuple-element.41.refs_9_), channel_id=1, source_target_pairs={{0,2},{1,3},{2,0},{3,1},{4,6},{5,7},{6,4},{7,5}} | collective-permute-start | bytes 835592 | tf_op jit(solution)/shard_map/ppermute | solution.py:316
  20.3 7.4 %attn_bwd.4 = (f32[32,128,256]{2,1,0:T(8,128)S(1)}, f32[512,128]{1,0:T(8,128)S(1)}, f32[512,128]{1,0:T(8,128)S(1)}, f32[512,128]{1,0:T(8,128)S(1)}, f32[512,128]{1,0:T(8,128)S(1)}) custom-call(s32[8,32]{1,0:T(8,128)S(1)} %get-tuple-element.32.refs_0_, bf16[2,4096,128]{2,1,0:T(8,128)(2,1)S(1)} %get-tuple-element.33.refs_1_, ...), custom_call_target="tpu_custom_call" | custom-call | flops 2000000000 | bytes 10000000 | tf_op jit(solution)/shard_map/attn_bwd/pallas_call | solution.py:348
  27.7 0.0 collective-permute-done.refs_6_
  27.7 3.3 %attn_bwd.5 = (f32[32,128,256]{2,1,0:T(8,128)S(1)}, f32[1088,128]{1,0:T(8,128)S(1)}, f32[1088,128]{1,0:T(8,128)S(1)}) custom-call(s32[8,32]{1,0:T(8,128)S(1)} %get-tuple-element.32.refs_0_, bf16[2,4096,128]{2,1,0:T(8,128)(2,1)S(1)} %get-tuple-element.33.refs_1_, ...), custom_call_target="tpu_custom_call", output_to_operand_aliasing={{0}: (8, {})} | custom-call | flops 2000000000 | bytes 10000000 | tf_op jit(solution)/shard_map/attn_bwd/pallas_call | solution.py:348
  31.0 0.0 copy-start
  31.0 0.0 copy-start.1
  31.0 6.5 %attn_bwd.6 = (f32[32,128,256]{2,1,0:T(8,128)S(1)}, f32[576,128]{1,0:T(8,128)S(1)}, f32[576,128]{1,0:T(8,128)S(1)}, f32[1088,128]{1,0:T(8,128)S(1)}, f32[1088,128]{1,0:T(8,128)S(1)}) custom-call(s32[8,32]{1,0:T(8,128)S(1)} %get-tuple-element.32.refs_0_, bf16[2,4096,128]{2,1,0:T(8,128)(2,1)S(1)} %get-tuple-element.33.refs_1_, ...), custom_call_target="tpu_custom_call", output_to_operand_aliasing={{0}: (10, {})} | custom-call | flops 2000000000 | bytes 10000000 | tf_op jit(solution)/shard_map/attn_bwd/pallas_call | solution.py:348
  37.5 7.4 %attn_bwd.7 = (f32[32,128,128]{2,1,0:T(8,128)S(1)}, f32[32,128,128]{2,1,0:T(8,128)S(1)}, f32[1088,128]{1,0:T(8,128)S(1)}, f32[1088,128]{1,0:T(8,128)S(1)}) custom-call(s32[8,32]{1,0:T(8,128)S(1)} %get-tuple-element.32.refs_0_, bf16[2,4096,128]{2,1,0:T(8,128)(2,1)S(1)} %get-tuple-element.33.refs_1_, bf16[2,4096,128]{2,1,0:T(8,128)(2,1)S(1)} %get-tuple-element.34.refs_2_, ...), custom_call_target="tpu_custom_call" | custom-call | flops 2000000000 | bytes 10000000 | tf_op jit(solution)/shard_map/attn_bwd/pallas_call | solution.py:348
  44.9 2.6 %collective-permute-start.2 = (f32[32,128,128]{2,1,0:T(8,128)S(1)}, f32[32,128,128]{2,1,0:T(8,128)S(1)}, u32[]{:S(2)}, u32[]{:S(2)}) collective-permute-start(f32[32,128,128]{2,1,0:T(8,128)S(1)} %get-tuple-element.48), channel_id=1, source_target_pairs={{0,1},{1,0},{2,3},{3,2},{4,5},{5,4},{6,7},{7,6}} | collective-permute-start | bytes 6291464 | tf_op jit(solution)/shard_map/ppermute | solution.py:316
  47.5 0.2 collective-permute-start.5
  47.7 3.0 %collective-permute-start.9 = (f32[1088,128]{1,0:T(8,128)S(1)}, f32[1088,128]{1,0:T(8,128)S(1)}, u32[]{:S(2)}, u32[]{:S(2)}) collective-permute-start(f32[1088,128]{1,0:T(8,128)S(1)} %get-tuple-element.58), channel_id=1, source_target_pairs={{0,4},{1,5},{2,6},{3,7},{4,0},{5,1},{6,2},{7,3}} | collective-permute-start | bytes 1671176 | tf_op jit(solution)/shard_map/ppermute | solution.py:316
  50.7 0.4 collective-permute-start.3
  51.1 0.4 collective-permute-start.7
  51.5 11.4 %collective-permute-done.5 = f32[1088,128]{1,0:T(8,128)S(1)} collective-permute-done((f32[1088,128]{1,0:T(8,128)S(1)}, f32[1088,128]{1,0:T(8,128)S(1)}, u32[]{:S(2)}, u32[]{:S(2)}) %collective-permute-start.5) | collective-permute-done | bytes 557088 | tf_op jit(solution)/shard_map/ppermute | solution.py:316
  63.0 0.1 add.6
  63.0 1.6 %collective-permute-start.6 = (f32[1088,128]{1,0:T(8,128)S(1)}, f32[1088,128]{1,0:T(8,128)S(1)}, u32[]{:S(2)}, u32[]{:S(2)}) collective-permute-start(f32[1088,128]{1,0:T(8,128)S(1)} %add.6), channel_id=1, source_target_pairs={{0,4},{1,5},{2,6},{3,7},{4,0},{5,1},{6,2},{7,3}} | collective-permute-start | bytes 1671176 | tf_op jit(solution)/shard_map/ppermute | solution.py:316
  64.7 0.0 collective-permute-done.9
  64.7 0.1 add.7
  64.7 1.6 %collective-permute-start.10 = (f32[1088,128]{1,0:T(8,128)S(1)}, f32[1088,128]{1,0:T(8,128)S(1)}, u32[]{:S(2)}, u32[]{:S(2)}) collective-permute-start(f32[1088,128]{1,0:T(8,128)S(1)} %add.7), channel_id=1, source_target_pairs={{0,2},{1,3},{2,0},{3,1},{4,6},{5,7},{6,4},{7,5}} | collective-permute-start | bytes 1671176 | tf_op jit(solution)/shard_map/ppermute | solution.py:316
  66.4 2.2 %collective-permute-done.3.ka_ref = f32[512,128]{1,0:T(8,128)S(1)} collective-permute-done((f32[512,128]{1,0:T(8,128)S(1)}, f32[512,128]{1,0:T(8,128)S(1)}, u32[]{:S(2)}, u32[]{:S(2)}) %collective-permute-start.3) | collective-permute-done | bytes 262176 | tf_op jit(solution)/shard_map/ppermute | solution.py:316
  68.6 0.2 collective-permute-start.4
  68.8 1.0 %collective-permute-done.7.va_ref = f32[512,128]{1,0:T(8,128)S(1)} collective-permute-done((f32[512,128]{1,0:T(8,128)S(1)}, f32[512,128]{1,0:T(8,128)S(1)}, u32[]{:S(2)}, u32[]{:S(2)}) %collective-permute-start.7) | collective-permute-done | bytes 262176 | tf_op jit(solution)/shard_map/ppermute | solution.py:316
  69.8 2.0 %collective-permute-start.8 = (f32[576,128]{1,0:T(8,128)S(1)}, f32[576,128]{1,0:T(8,128)S(1)}, u32[]{:S(2)}, u32[]{:S(2)}) collective-permute-start(f32[576,128]{1,0:T(8,128)S(1)} %get-tuple-element.56), channel_id=1, source_target_pairs={{0,4},{1,5},{2,6},{3,7},{4,0},{5,1},{6,2},{7,3}} | collective-permute-start | bytes 884744 | tf_op jit(solution)/shard_map/ppermute | solution.py:316
  71.8 14.1 %collective-permute-done.4.kb_ref = f32[576,128]{1,0:T(8,128)S(1)} collective-permute-done((f32[576,128]{1,0:T(8,128)S(1)}, f32[576,128]{1,0:T(8,128)S(1)}, u32[]{:S(2)}, u32[]{:S(2)}) %collective-permute-start.4) | collective-permute-done | bytes 294944 | tf_op jit(solution)/shard_map/ppermute | solution.py:316
  85.9 1.2 %collective-permute-done.8.vb_ref = f32[576,128]{1,0:T(8,128)S(1)} collective-permute-done((f32[576,128]{1,0:T(8,128)S(1)}, f32[576,128]{1,0:T(8,128)S(1)}, u32[]{:S(2)}, u32[]{:S(2)}) %collective-permute-start.8) | collective-permute-done | bytes 294944 | tf_op jit(solution)/shard_map/ppermute | solution.py:316
  87.1 0.0 collective-permute-done.6.lk_ref
  87.1 0.0 collective-permute-done.10.lv_ref
  87.1 1.1 %sum_kv.1 = (f32[1088,128]{1,0:T(8,128)}, f32[1088,128]{1,0:T(8,128)}) custom-call(f32[1088,128]{1,0:T(8,128)S(1)} %get-tuple-element.49.dk_ref, f32[512,128]{1,0:T(8,128)S(1)} %collective-permute-done.3.ka_ref, f32[576,128]{1,0:T(8,128)S(1)} %collective-permute-done.4.kb_ref, f32[1088,128]{1,0:T(8,128)S(1)} %collective-permute-done.6.lk_ref, ...), custom_call_target="tpu_custom_call" | custom-call | flops 2000000000 | bytes 10000000 | tf_op jit(solution)/shard_map/sum_kv/pallas_call | solution.py:394
  88.3 0.0 collective-permute-done.2.got_ref
  88.3 1.9 %finish_dq.1 = bf16[4096,128]{1,0:T(8,128)(2,1)} custom-call(f32[32,128,128]{2,1,0:T(8,128)S(1)} %get-tuple-element.47.own_ref, f32[32,128,128]{2,1,0:T(8,128)S(1)} %collective-permute-done.2.got_ref), custom_call_target="tpu_custom_call" | custom-call | flops 2000000000 | bytes 10000000 | tf_op jit(solution)/shard_map/finish_dq/pallas_call | solution.py:390
  (3 shorter events, 0.0 us)
Async XLA Ops:
  18.2 9.4 %collective-permute-start = (bf16[1088,128]{1,0:T(8,128)(2,1)S(1)}, bf16[1088,128]{1,0:T(8,128)(2,1)S(1)}, u32[]{:S(2)}, u32[]{:S(2)}) collective-permute-start(bf16[1088,128]{1,0:T(8,128)(2,1)S(1)} %get-tuple-element.38.refs_6_), channel_id=1, source_target_pairs={{0,4},{1,5},{2,6},{3,7},{4,0},{5,1},{6,2},{7,3}} | collective-permute-start | bytes 835592 | tf_op jit(solution)/shard_map/ppermute | solution.py:316
  19.2 8.5 %collective-permute-start.1 = (bf16[1088,128]{1,0:T(8,128)(2,1)S(1)}, bf16[1088,128]{1,0:T(8,128)(2,1)S(1)}, u32[]{:S(2)}, u32[]{:S(2)}) collective-permute-start(bf16[1088,128]{1,0:T(8,128)(2,1)S(1)} %get-tuple-element.41.refs_9_), channel_id=1, source_target_pairs={{0,2},{1,3},{2,0},{3,1},{4,6},{5,7},{6,4},{7,5}} | collective-permute-start | bytes 835592 | tf_op jit(solution)/shard_map/ppermute | solution.py:316
  31.0 6.5 %copy-start = (bf16[1088,1,128]{2,0,1:T(8,128)(2,1)S(1)}, bf16[1088,1,128]{2,0,1:T(8,128)(2,1)}, u32[]{:S(2)}) copy-start(bf16[1088,1,128]{2,0,1:T(8,128)(2,1)} %param.11) | copy-start | bytes 835588
  31.0 6.5 %copy-start.1 = (bf16[1088,1,128]{2,0,1:T(8,128)(2,1)S(1)}, bf16[1088,1,128]{2,0,1:T(8,128)(2,1)}, u32[]{:S(2)}) copy-start(bf16[1088,1,128]{2,0,1:T(8,128)(2,1)} %param.12) | copy-start | bytes 835588
  44.9 43.4 %collective-permute-start.2 = (f32[32,128,128]{2,1,0:T(8,128)S(1)}, f32[32,128,128]{2,1,0:T(8,128)S(1)}, u32[]{:S(2)}, u32[]{:S(2)}) collective-permute-start(f32[32,128,128]{2,1,0:T(8,128)S(1)} %get-tuple-element.48), channel_id=1, source_target_pairs={{0,1},{1,0},{2,3},{3,2},{4,5},{5,4},{6,7},{7,6}} | collective-permute-start | bytes 6291464 | tf_op jit(solution)/shard_map/ppermute | solution.py:316
  47.5 15.5 %collective-permute-start.5 = (f32[1088,128]{1,0:T(8,128)S(1)}, f32[1088,128]{1,0:T(8,128)S(1)}, u32[]{:S(2)}, u32[]{:S(2)}) collective-permute-start(f32[1088,128]{1,0:T(8,128)S(1)} %get-tuple-element.53), channel_id=1, source_target_pairs={{0,2},{1,3},{2,0},{3,1},{4,6},{5,7},{6,4},{7,5}} | collective-permute-start | bytes 1671176 | tf_op jit(solution)/shard_map/ppermute | solution.py:316
  47.7 17.0 %collective-permute-start.9 = (f32[1088,128]{1,0:T(8,128)S(1)}, f32[1088,128]{1,0:T(8,128)S(1)}, u32[]{:S(2)}, u32[]{:S(2)}) collective-permute-start(f32[1088,128]{1,0:T(8,128)S(1)} %get-tuple-element.58), channel_id=1, source_target_pairs={{0,4},{1,5},{2,6},{3,7},{4,0},{5,1},{6,2},{7,3}} | collective-permute-start | bytes 1671176 | tf_op jit(solution)/shard_map/ppermute | solution.py:316
  50.7 17.9 %collective-permute-start.3 = (f32[512,128]{1,0:T(8,128)S(1)}, f32[512,128]{1,0:T(8,128)S(1)}, u32[]{:S(2)}, u32[]{:S(2)}) collective-permute-start(f32[512,128]{1,0:T(8,128)S(1)} %get-tuple-element.50), channel_id=1, source_target_pairs={{0,2},{1,3},{2,0},{3,1},{4,6},{5,7},{6,4},{7,5}} | collective-permute-start | bytes 786440 | tf_op jit(solution)/shard_map/ppermute | solution.py:316
  51.1 18.7 %collective-permute-start.7 = (f32[512,128]{1,0:T(8,128)S(1)}, f32[512,128]{1,0:T(8,128)S(1)}, u32[]{:S(2)}, u32[]{:S(2)}) collective-permute-start(f32[512,128]{1,0:T(8,128)S(1)} %get-tuple-element.55), channel_id=1, source_target_pairs={{0,4},{1,5},{2,6},{3,7},{4,0},{5,1},{6,2},{7,3}} | collective-permute-start | bytes 786440 | tf_op jit(solution)/shard_map/ppermute | solution.py:316
  63.0 24.1 %collective-permute-start.6 = (f32[1088,128]{1,0:T(8,128)S(1)}, f32[1088,128]{1,0:T(8,128)S(1)}, u32[]{:S(2)}, u32[]{:S(2)}) collective-permute-start(f32[1088,128]{1,0:T(8,128)S(1)} %add.6), channel_id=1, source_target_pairs={{0,4},{1,5},{2,6},{3,7},{4,0},{5,1},{6,2},{7,3}} | collective-permute-start | bytes 1671176 | tf_op jit(solution)/shard_map/ppermute | solution.py:316
  64.7 22.4 %collective-permute-start.10 = (f32[1088,128]{1,0:T(8,128)S(1)}, f32[1088,128]{1,0:T(8,128)S(1)}, u32[]{:S(2)}, u32[]{:S(2)}) collective-permute-start(f32[1088,128]{1,0:T(8,128)S(1)} %add.7), channel_id=1, source_target_pairs={{0,2},{1,3},{2,0},{3,1},{4,6},{5,7},{6,4},{7,5}} | collective-permute-start | bytes 1671176 | tf_op jit(solution)/shard_map/ppermute | solution.py:316
  68.6 17.3 %collective-permute-start.4 = (f32[576,128]{1,0:T(8,128)S(1)}, f32[576,128]{1,0:T(8,128)S(1)}, u32[]{:S(2)}, u32[]{:S(2)}) collective-permute-start(f32[576,128]{1,0:T(8,128)S(1)} %get-tuple-element.51), channel_id=1, source_target_pairs={{0,2},{1,3},{2,0},{3,1},{4,6},{5,7},{6,4},{7,5}} | collective-permute-start | bytes 884744 | tf_op jit(solution)/shard_map/ppermute | solution.py:316
  69.8 17.3 %collective-permute-start.8 = (f32[576,128]{1,0:T(8,128)S(1)}, f32[576,128]{1,0:T(8,128)S(1)}, u32[]{:S(2)}, u32[]{:S(2)}) collective-permute-start(f32[576,128]{1,0:T(8,128)S(1)} %get-tuple-element.56), channel_id=1, source_target_pairs={{0,4},{1,5},{2,6},{3,7},{4,0},{5,1},{6,2},{7,3}} | collective-permute-start | bytes 884744 | tf_op jit(solution)/shard_map/ppermute | solution.py:316
